TPU v7x, 32 devices: a whole 2x2x4 slice. The times are simulated.
32 devices in a mesh: replica: 16 (over z, y, core), shard: 2 (over x).
Axes of the slice: x: 2, y: 2, z: 4, core: 2. Of those that a mesh axis runs over, the one named last changes fastest.
Arguments:
- weight: bfloat16 [256, 8192], P(None, 'shard'), may hold values from -6 to 6
- momentum: float32 [16, 256, 8192], P('replica', None, 'shard'), may hold values from -6 to 6
- grad: bfloat16 [16, 256, 8192], P('replica', None, 'shard'), may hold values from -6 to 6
- positions: int32 [16, 4, 128, 32], P('replica', None, 'shard'), may hold values from 0 to 4095, as said below
Outputs:
- kept_state: float32 [16, 256, 8192], P('replica', None, 'shard')
- direction: bfloat16 [256, 8192], P(None, 'shard')
- new_weight: bfloat16 [256, 8192], replicated
Inputs may be any that keep to these rules, and one draw needn't show every extreme that they name: The 32 positions of one block on one replica are distinct; replicas choose independently.
All inputs are finite; a program needn't handle non-finite values.
Results may differ from a plain program's by a relative error of at most 0.001.
Values may be sent and summed in bfloat16 or wider, within the bound.
A program may use at most 128 MiB of HBM per device.

v0:
```python
import functools
import math

import jax
import jax.numpy as jnp
import numpy as np
from jax import lax
from jax.experimental import pallas as pl
from jax.experimental.pallas import tpu as pltpu
from jax.sharding import PartitionSpec as P

GROUP = 64
LANES = 128
WIDE = 256

beta_decay = 0.9
step_rate = 0.02

f32, bf16 = jnp.float32, jnp.bfloat16
MESH = pl.DeviceIdType.MESH


def basis_parts(blocks, transposed):
    k = np.arange(GROUP, dtype=np.float64)[:, None]
    i = np.arange(GROUP, dtype=np.float64)[None, :]
    scale = np.where(k == 0, math.sqrt(1.0 / GROUP), math.sqrt(2.0 / GROUP))
    c = scale * np.cos(math.pi * (2.0 * i + 1.0) * k / (2.0 * GROUP))
    if transposed:
        c = c.T
    full = np.kron(np.eye(blocks), c).astype(np.float32)
    high = full.astype(bf16)
    low = (full - high.astype(np.float32)).astype(bf16)
    return np.stack([high, low])


def split(x):
    high = x.astype(bf16)
    return high, (x - high.astype(f32)).astype(bf16)


def dot(a, b):
    return jnp.dot(a, b, preferred_element_type=f32)


def dot_t(a, b):
    return lax.dot_general(a, b, (((1,), (1,)), ((), ())), preferred_element_type=f32)


def left(m, x):
    high, low = split(x)
    return dot(m[0], high) + (dot(m[0], low) + dot(m[1], high))


def right(x, m):
    high, low = split(x)
    return dot(high, m[0]) + (dot(low, m[0]) + dot(high, m[1]))


def down(rows):
    return lax.broadcasted_iota(jnp.int32, (rows, LANES), 0).astype(f32)


def lane_offset(topk):
    lane = lax.broadcasted_iota(jnp.int32, (1, LANES), 1)
    return (lane // topk * GROUP).astype(f32)


def place(pos, topk):
    a = jnp.floor(pos * (1.0 / GROUP))
    return a, pos - a * GROUP + lane_offset(topk)


def own_kernel(nx, topk, mom, grad, pos, lf, rt, li, ri, kept, sent):
    moved = beta_decay * mom[0] + grad[0].astype(f32)
    coeff = right(left(lf, moved), rt)
    spots = pos[0]
    a, b = place(spots, topk)
    rows, cols = down(GROUP), down(WIDE)
    picked, own = [], []
    for x in range(nx):
        part = coeff[x * GROUP : (x + 1) * GROUP]
        at_row = rows == a[x : x + 1]
        hot_a = jnp.where(at_row, 1.0, 0.0).astype(bf16)
        hot_b = jnp.where(cols == b[x : x + 1], 1.0, 0.0).astype(bf16)
        own.append(part * dot_t(hot_a, hot_b))
        high, low = split(part)
        found = dot(jnp.concatenate([high, low], axis=0), hot_b)
        found = found[:GROUP] + found[GROUP:]
        picked.append(jnp.sum(jnp.where(at_row, found, 0.0), axis=0, keepdims=True))
    kept[0] = moved - right(left(li, jnp.concatenate(own, axis=0)), ri)
    sent[0] = jnp.concatenate(picked + [spots], axis=0)


def own_part(mom, grad, pos, topk, interpret=False):
    _, rows, width = mom.shape
    nx = rows // GROUP
    steps = width // WIDE
    blocks = WIDE // GROUP
    whole = lambda n: pl.BlockSpec((2, n, n), lambda g: (0, 0, 0))
    return pl.pallas_call(
        functools.partial(own_kernel, nx, topk),
        grid=(steps,),
        in_specs=[
            pl.BlockSpec((1, rows, WIDE), lambda g: (0, 0, g)),
            pl.BlockSpec((1, rows, WIDE), lambda g: (0, 0, g)),
            pl.BlockSpec((1, nx, LANES), lambda g: (g, 0, 0)),
            whole(rows), whole(WIDE), whole(rows), whole(WIDE),
        ],
        out_specs=[
            pl.BlockSpec((1, rows, WIDE), lambda g: (0, 0, g)),
            pl.BlockSpec((1, 2 * nx, LANES), lambda g: (g, 0, 0)),
        ],
        out_shape=[
            jax.ShapeDtypeStruct((1, rows, width), f32),
            jax.ShapeDtypeStruct((steps, 2 * nx, LANES), f32),
        ],
        interpret=interpret,
        name="own_part",
    )(
        mom, grad, pos,
        basis_parts(nx, False), basis_parts(blocks, True),
        basis_parts(nx, True), basis_parts(blocks, False),
    )


def swap_kernel(reps, shards, mine, got, send_sem, recv_sem, own_sem):
    r, s = lax.axis_index("replica"), lax.axis_index("shard")
    me = r * shards + s
    total = reps * shards
    keep = pltpu.make_async_copy(mine.at[lax.rem(r, 2)], got.at[s, r], own_sem)
    keep.start()

    def push(step):
        to = lax.rem(me + step, total)
        to_r, to_s = to // shards, lax.rem(to, shards)
        return pltpu.make_async_remote_copy(
            src_ref=mine.at[lax.rem(to_r, 2)],
            dst_ref=got.at[s, r],
            send_sem=send_sem.at[step],
            recv_sem=recv_sem.at[step],
            device_id=(to_r, to_s),
            device_id_type=MESH,
        )

    def come(step):
        of = lax.rem(me - step + total, total)
        of_r, of_s = of // shards, lax.rem(of, shards)
        return pltpu.make_async_remote_copy(
            src_ref=mine.at[0],
            dst_ref=got.at[of_s, of_r],
            send_sem=send_sem.at[step],
            recv_sem=recv_sem.at[step],
            device_id=(of_r, of_s),
            device_id_type=MESH,
        )

    @pl.loop(1, total)
    def _(step):
        push(step).start()

    @pl.loop(1, total)
    def _(step):
        push(step).wait_send()
        come(step).wait_recv()

    keep.wait()


def swap(mine, reps, shards):
    return pl.pallas_call(
        functools.partial(swap_kernel, reps, shards),
        in_specs=[pl.BlockSpec(memory_space=pltpu.VMEM)],
        out_specs=pl.BlockSpec(memory_space=pltpu.VMEM),
        out_shape=jax.ShapeDtypeStruct((shards, reps) + mine.shape[1:], f32),
        scratch_shapes=[
            pltpu.SemaphoreType.DMA((reps * shards,)),
            pltpu.SemaphoreType.DMA((reps * shards,)),
            pltpu.SemaphoreType.DMA,
        ],
        compiler_params=pltpu.CompilerParams(has_side_effects=True),
        name="swap",
    )(mine)


def sum_kernel(nx, topk, reps, _, data, weight, li, ri, smooth_out, weight_out):
    rows, cols = down(GROUP), down(WIDE)
    tiles = []
    for x in range(nx):
        lefts, rights = [], []
        for r in range(reps):
            tile = data[0, r, 0]
            a, b = place(tile[nx + x : nx + x + 1], topk)
            high, low = split(tile[x : x + 1])
            at_row = rows == a
            lefts.append(jnp.concatenate([
                jnp.where(at_row, high.astype(f32), 0.0).astype(bf16),
                jnp.where(at_row, low.astype(f32), 0.0).astype(bf16),
            ], axis=0))
            rights.append(jnp.where(cols == b, 1.0, 0.0).astype(bf16))
        both = dot_t(jnp.concatenate(lefts, axis=1), jnp.concatenate(rights, axis=1))
        tiles.append(both[:GROUP] + both[GROUP:])
    smooth = jnp.tanh(right(left(li, jnp.concatenate(tiles, axis=0)), ri))
    smooth_out[...] = smooth.astype(bf16)
    weight_out[...] = (weight[...].astype(f32) - step_rate * smooth).astype(bf16)


def sum_part(shard, data, weight, topk, interpret=False):
    rows, width = weight.shape
    nx = rows // GROUP
    reps = data.shape[1]
    blocks = WIDE // GROUP
    column = pl.BlockSpec((rows, WIDE), lambda g, s: (0, g))
    whole = lambda n: pl.BlockSpec((2, n, n), lambda g, s: (0, 0, 0))
    return pl.pallas_call(
        functools.partial(sum_kernel, nx, topk, reps),
        grid_spec=pltpu.PrefetchScalarGridSpec(
            num_scalar_prefetch=1,
            grid=(width // WIDE,),
            in_specs=[
                pl.BlockSpec((1, reps, 1, 2 * nx, LANES), lambda g, s: (s[0], 0, g, 0, 0)),
                column, whole(rows), whole(WIDE),
            ],
            out_specs=[column, column],
        ),
        out_shape=[jax.ShapeDtypeStruct((rows, width), bf16)] * 2,
        interpret=interpret,
        name="sum_part",
    )(shard, data, weight, basis_parts(nx, True), basis_parts(blocks, False))


def per_device(reps, shards, weight, momentum, grad, positions):
    rows, width = weight.shape
    _, nx, ny, topk = positions.shape
    half = width // 2
    steps = width // WIDE
    r, s = lax.axis_index("replica"), lax.axis_index("shard")
    core = lax.rem(r, 2)

    mine_w = lax.dynamic_slice(weight, (0, core * half), (rows, half))
    weights = [mine_w] + [
        lax.ppermute(mine_w, "shard", [(i, (i + d) % shards) for i in range(shards)])
        for d in range(1, shards)
    ]

    pos = positions[0].astype(f32).reshape(nx, steps, LANES).transpose(1, 0, 2)
    kept, sent = own_part(momentum, grad, pos, topk)
    got = swap(sent.reshape(2, steps // 2, 2 * nx, LANES), reps, shards)

    pairs = [(i, i ^ 1) for i in range(reps)]
    flip = lambda x: lax.ppermute(x, "replica", pairs)
    order = lambda a, b: [jnp.where(core == 0, a, b), jnp.where(core == 0, b, a)]
    pieces, direction = [], None
    for d in range(shards):
        of = lax.rem(s - d + shards, shards)
        smooth, updated = sum_part(of.reshape(1).astype(jnp.int32), got, weights[d], topk)
        if d == 0:
            direction = jnp.concatenate(order(smooth, flip(smooth)), axis=1)
        pieces.append((updated, flip(updated)))

    columns = []
    for t in range(shards):
        d = lax.rem(s - t + shards, shards)
        a, b = pieces[0]
        for e in range(1, shards):
            a = jnp.where(d == e, pieces[e][0], a)
            b = jnp.where(d == e, pieces[e][1], b)
        columns += order(a, b)
    return (kept, direction, jnp.concatenate(columns, axis=1))


def solution(mesh):
    reps, shards = mesh.shape["replica"], mesh.shape["shard"]
    in_specs = (
        P(None, "shard"),
        P("replica", None, "shard"),
        P("replica", None, "shard"),
        P("replica", None, "shard", None),
    )
    out_specs = (P("replica", None, "shard"), P(None, "shard"), P())
    return jax.shard_map(
        functools.partial(per_device, reps, shards),
        mesh=mesh, in_specs=in_specs, out_specs=out_specs, check_vma=False,
    )
```

profile of v0, /device:TPU:15, one launch (start us, length us, event | category | flops | bytes accessed | tf_op | source)
XLA Modules:
  0.0 106.7 jit_solution(17722004219141447098)
XLA Ops:
  0.6 0.0 copy-start
  0.7 1.6 %copy-done = bf16[256,4096]{1,0:T(8,128)(2,1)S(1)} copy-done((bf16[256,4096]{1,0:T(8,128)(2,1)S(1)}, bf16[256,4096]{1,0:T(8,128)(2,1)}, u32[]{:S(2)}) %copy-start) | copy-done | bytes 2097176
  2.2 0.1 constant_dynamic-slice_fusion.weight
  2.3 0.0 copy-start.1
  2.3 0.3 collective-permute-start.1
  2.6 0.9 convert_element_type.7
  3.5 0.1 copy.15
  3.6 0.1 convert_element_type.8
  3.7 0.6 copy.18
  4.3 21.9 %own_part.1 = (f32[1,256,4096]{2,1,0:T(8,128)}, f32[16,8,128]{2,1,0:T(8,128)}) custom-call(f32[1,256,4096]{2,1,0:T(8,128)} %mom.1, bf16[1,256,4096]{2,1,0:T(8,128)(2,1)} %grad.1, f32[16,4,128]{2,1,0:T(4,128)} %bitcast.8, bf16[2,256,256]{2,1,0:T(8,128)(2,1)} %constant.30.clone.lf.ri, bf16[2,256,256]{2,1,0:T(8,128)(2,1)} %constant.31.clone.rt.li, ...), custom_call_target="tpu_custom_call" | custom-call | tf_op jit(solution)/shard_map/own_part/pallas_call | solution.py:100
  26.3 34.3 %swap.1.data = f32[2,16,8,8,128]{4,3,2,1,0:T(8,128)} custom-call(f32[2,8,8,128]{3,2,1,0:T(8,128)} %bitcast.9), custom_call_target="tpu_custom_call" | custom-call | tf_op jit(solution)/shard_map/swap/pallas_call | solution.py:170
  60.6 0.0 copy-done.1
  60.6 19.1 %sum_part.2 = (bf16[256,2048]{1,0:T(8,128)(2,1)}, bf16[256,2048]{1,0:T(8,128)(2,1)}) custom-call(s32[1]{0:T(128)} %bitcast.1._, f32[2,16,8,8,128]{4,3,2,1,0:T(8,128)} %swap.1.data, bf16[256,2048]{1,0:T(8,128)(2,1)} %copy-done.1, bf16[2,256,256]{2,1,0:T(8,128)(2,1)} %constant.31.clone.rt.li, bf16[2,256,256]{2,1,0:T(8,128)(2,1)} %constant.30.clone.lf.ri), custom_call_target="tpu_custom_call" | custom-call | tf_op jit(solution)/shard_map/sum_part/pallas_call | solution.py:214
  79.8 0.0 collective-permute-start
  79.8 0.5 collective-permute-start.3
  80.3 0.0 collective-permute-done.1.weight
  80.3 19.1 %sum_part.3 = (bf16[256,2048]{1,0:T(8,128)(2,1)}, bf16[256,2048]{1,0:T(8,128)(2,1)}) custom-call(s32[1]{0:T(128)} %bitcast.3._, f32[2,16,8,8,128]{4,3,2,1,0:T(8,128)} %swap.1.data, bf16[256,2048]{1,0:T(8,128)(2,1)} %collective-permute-done.1.weight, bf16[2,256,256]{2,1,0:T(8,128)(2,1)} %constant.31.clone.rt.li, bf16[2,256,256]{2,1,0:T(8,128)(2,1)} %constant.30.clone.lf.ri), custom_call_target="tpu_custom_call" | custom-call | tf_op jit(solution)/shard_map/sum_part/pallas_call | solution.py:214
  99.4 0.0 copy-start.2
  99.4 0.0 copy-start.3
  99.4 0.1 collective-permute-start.2
  99.5 0.0 collective-permute-done
  99.6 1.8 %broadcast_select_fusion.9 = (bf16[256,2048]{1,0:T(8,128)(2,1)S(1)}, bf16[256,2048]{1,0:T(8,128)(2,1)S(1)}) fusion(bf16[256,2048]{1,0:T(8,128)(2,1)} %get-tuple-element.10, bf16[256,2048]{1,0:T(8,128)(2,1)} %collective-permute-done, pred[]{:T(512)S(6)} %eq.6), kind=kLoop, calls=%fused_computation.11 | loop fusion | flops 1048576 | bytes 4194305 | tf_op jit(solution)/shard_map/jit(_where)/select_n | solution.py:251
  101.4 1.5 %pad_maximum_fusion.1 = bf16[256,4096]{1,0:T(8,128)(2,1)} fusion(bf16[256,2048]{1,0:T(8,128)(2,1)S(1)} %get-tuple-element.18, bf16[256,2048]{1,0:T(8,128)(2,1)S(1)} %get-tuple-element.17), kind=kLoop, calls=%fused_computation.1 | loop fusion | flops 4194304 | bytes 4194304 | tf_op jit(solution)/shard_map/concatenate | solution.py:257
  102.9 0.0 collective-permute-done.3
  102.9 0.0 collective-permute-done.2
  102.9 0.0 copy-done.2
  102.9 0.0 copy-done.3
  102.9 1.6 %broadcast_select_fusion.7 = (bf16[256,2048]{1,0:T(8,128)(2,1)S(1)}, bf16[256,2048]{1,0:T(8,128)(2,1)S(1)}, bf16[256,2048]{1,0:T(8,128)(2,1)S(1)}, bf16[256,2048]{1,0:T(8,128)(2,1)S(1)}) fusion(pred[]{:T(512)S(6)} %eq.6, bf16[256,2048]{1,0:T(8,128)(2,1)S(1)} %copy-done.3, bf16[256,2048]{1,0:T(8,128)(2,1)S(1)} %copy-done.2, pred[]{:T(512)S(6)} %eq.7, ...), kind=kLoop, calls=%fused_computation.9 | loop fusion | flops 4194304 | bytes 8388611 | tf_op jit(solution)/shard_map/jit(_where)/select_n | solution.py:251
  104.5 2.2 %pad_maximum_fusion = bf16[256,8192]{1,0:T(8,128)(2,1)} fusion(bf16[256,2048]{1,0:T(8,128)(2,1)S(1)} %get-tuple-element.16, bf16[256,2048]{1,0:T(8,128)(2,1)S(1)} %get-tuple-element.15, bf16[256,2048]{1,0:T(8,128)(2,1)S(1)} %get-tuple-element.14, bf16[256,2048]{1,0:T(8,128)(2,1)S(1)} %get-tuple-element.13), kind=kLoop, calls=%fused_computation | loop fusion | flops 16777216 | bytes 8388608 | tf_op jit(solution)/shard_map/concatenate | solution.py:268
Async XLA Ops:
  0.6 1.6 %copy-start = (bf16[256,4096]{1,0:T(8,128)(2,1)S(1)}, bf16[256,4096]{1,0:T(8,128)(2,1)}, u32[]{:S(2)}) copy-start(bf16[256,4096]{1,0:T(8,128)(2,1)} %param.12) | copy-start | bytes 6291460
  2.3 58.3 %copy-start.1 = (bf16[256,2048]{1,0:T(8,128)(2,1)}, bf16[256,2048]{1,0:T(8,128)(2,1)S(1)}, u32[]{:S(2)}) copy-start(bf16[256,2048]{1,0:T(8,128)(2,1)S(1)} %constant_dynamic-slice_fusion.weight) | copy-start | bytes 3145732
  2.3 78.0 %collective-permute-start.1 = (bf16[256,2048]{1,0:T(8,128)(2,1)S(1)}, bf16[256,2048]{1,0:T(8,128)(2,1)}, u32[]{:S(2)}, u32[]{:S(2)}) collective-permute-start(bf16[256,2048]{1,0:T(8,128)(2,1)S(1)} %constant_dynamic-slice_fusion.weight), channel_id=1, source_target_pairs={{0,1},{1,0},{2,3},{3,2},{4,5},{5,4},{6,7},{7,6},{8,9},{9,8},{10,11... | collective-permute-start | bytes 3145736 | tf_op jit(solution)/shard_map/ppermute | solution.py:241
  79.8 19.8 %collective-permute-start = (bf16[256,2048]{1,0:T(8,128)(2,1)}, bf16[256,2048]{1,0:T(8,128)(2,1)}, u32[]{:S(2)}, u32[]{:S(2)}) collective-permute-start(bf16[256,2048]{1,0:T(8,128)(2,1)} %get-tuple-element.10), channel_id=1, source_target_pairs={{0,2},{2,0},{4,6},{6,4},{8,10},{10,8},{12,14},{14,12},{16,18},{18,... | collective-permute-start | bytes 3145736 | tf_op jit(solution)/shard_map/ppermute | solution.py:250
  79.8 23.1 %collective-permute-start.3 = (bf16[256,2048]{1,0:T(8,128)(2,1)}, bf16[256,2048]{1,0:T(8,128)(2,1)}, u32[]{:S(2)}, u32[]{:S(2)}) collective-permute-start(bf16[256,2048]{1,0:T(8,128)(2,1)} %get-tuple-element.12), channel_id=1, source_target_pairs={{0,2},{2,0},{4,6},{6,4},{8,10},{10,8},{12,14},{14,12},{16,18},{18,... | collective-permute-start | bytes 3145736 | tf_op jit(solution)/shard_map/ppermute | solution.py:250
  99.4 3.5 %copy-start.2 = (bf16[256,2048]{1,0:T(8,128)(2,1)S(1)}, bf16[256,2048]{1,0:T(8,128)(2,1)}, u32[]{:S(2)}) copy-start(bf16[256,2048]{1,0:T(8,128)(2,1)} %get-tuple-element.12) | copy-start | bytes 3145732
  99.4 3.5 %copy-start.3 = (bf16[256,2048]{1,0:T(8,128)(2,1)S(1)}, bf16[256,2048]{1,0:T(8,128)(2,1)}, u32[]{:S(2)}) copy-start(bf16[256,2048]{1,0:T(8,128)(2,1)} %get-tuple-element.11) | copy-start | bytes 3145732
  99.4 3.5 %collective-permute-start.2 = (bf16[256,2048]{1,0:T(8,128)(2,1)}, bf16[256,2048]{1,0:T(8,128)(2,1)S(1)}, u32[]{:S(2)}, u32[]{:S(2)}) collective-permute-start(bf16[256,2048]{1,0:T(8,128)(2,1)} %get-tuple-element.11), channel_id=1, source_target_pairs={{0,2},{2,0},{4,6},{6,4},{8,10},{10,8},{12,14},{14,12},{16,18},{18,... | collective-permute-start | bytes 3145736 | tf_op jit(solution)/shard_map/ppermute | solution.py:250
where the time goes:
time: 107 us
  Pallas kernels  94.5 us (88%)
  other arithmetic  8.03 us (8%)
  local copies, waits for them, and re-layouts  2.47 us (2%)
    pallas_call x2, Pallas kernels, sum_part(): pl.pallas_call(functools.partial(sum_kernel, nx, topk, reps), grid_spec=p...  38.3 us
    pallas_call x1, Pallas kernels, swap(): pl.pallas_call(functools.partial(swap_kernel, reps, shards), in_specs=[pl...  34.3 us
    pallas_call x1, Pallas kernels, own_part(): pl.pallas_call(functools.partial(own_kernel, nx, topk), grid=(steps,), in...  21.9 us
    select_n x2, other arithmetic, per_device(): jnp.where(core == 0, a, b)  3.38 us
    concatenate x1, other arithmetic, per_device(): return (kept, direction, jnp.concatenate(columns, axis=1))  2.23 us
  transfers between devices with their start and end apart: 4, of which 0 were waited for; matrix products, arithmetic and copies ran while one was open for 5% of the time, Pallas kernels for 89%

commit v1 on v0

--- a/solution.py
+++ b/solution.py
@@ -12,6 +12,7 @@
 GROUP = 64
 LANES = 128
 WIDE = 256
+PAIR = 128
 
 beta_decay = 0.9
 step_rate = 0.02
@@ -20,17 +21,28 @@
 MESH = pl.DeviceIdType.MESH
 
 
-def basis_parts(blocks, transposed):
+def basis():
     k = np.arange(GROUP, dtype=np.float64)[:, None]
     i = np.arange(GROUP, dtype=np.float64)[None, :]
     scale = np.where(k == 0, math.sqrt(1.0 / GROUP), math.sqrt(2.0 / GROUP))
-    c = scale * np.cos(math.pi * (2.0 * i + 1.0) * k / (2.0 * GROUP))
-    if transposed:
-        c = c.T
-    full = np.kron(np.eye(blocks), c).astype(np.float32)
+    return scale * np.cos(math.pi * (2.0 * i + 1.0) * k / (2.0 * GROUP))
+
+
+def halves(c):
+    full = np.kron(np.eye(PAIR // GROUP), c).astype(np.float32)
     high = full.astype(bf16)
     low = (full - high.astype(np.float32)).astype(bf16)
-    return np.stack([high, low])
+    return high, low
+
+
+def left_basis(c):
+    high, low = halves(c)
+    return np.block([[high, high], [low, low]])
+
+
+def right_basis(c):
+    high, low = halves(c)
+    return np.block([[high, low], [high, low]])
 
 
 def split(x):
@@ -48,12 +60,22 @@
 
 def left(m, x):
     high, low = split(x)
-    return dot(m[0], high) + (dot(m[0], low) + dot(m[1], high))
+    parts = []
+    for at in range(0, x.shape[0], PAIR):
+        both = dot(m, jnp.concatenate([high[at : at + PAIR], low[at : at + PAIR]], axis=0))
+        parts.append(both[:PAIR] + both[PAIR:])
+    return jnp.concatenate(parts, axis=0)
 
 
 def right(x, m):
     high, low = split(x)
-    return dot(high, m[0]) + (dot(low, m[0]) + dot(high, m[1]))
+    rows = x.shape[0]
+    ats = range(0, x.shape[1], PAIR)
+    both = dot(jnp.concatenate([
+        jnp.concatenate([high[:, at : at + PAIR], low[:, at : at + PAIR]], axis=1) for at in ats
+    ], axis=0), m)
+    both = both[:, :PAIR] + both[:, PAIR:]
+    return jnp.concatenate([both[i * rows : (i + 1) * rows] for i in range(len(ats))], axis=1)
 
 
 def down(rows):
@@ -71,6 +93,7 @@
 
 
 def own_kernel(nx, topk, mom, grad, pos, lf, rt, li, ri, kept, sent):
+    lf, rt, li, ri = lf[...], rt[...], li[...], ri[...]
     moved = beta_decay * mom[0] + grad[0].astype(f32)
     coeff = right(left(lf, moved), rt)
     spots = pos[0]
@@ -95,8 +118,7 @@
     _, rows, width = mom.shape
     nx = rows // GROUP
     steps = width // WIDE
-    blocks = WIDE // GROUP
-    whole = lambda n: pl.BlockSpec((2, n, n), lambda g: (0, 0, 0))
+    whole = pl.BlockSpec((2 * PAIR, 2 * PAIR), lambda g: (0, 0))
     return pl.pallas_call(
         functools.partial(own_kernel, nx, topk),
         grid=(steps,),
@@ -104,7 +126,7 @@
             pl.BlockSpec((1, rows, WIDE), lambda g: (0, 0, g)),
             pl.BlockSpec((1, rows, WIDE), lambda g: (0, 0, g)),
             pl.BlockSpec((1, nx, LANES), lambda g: (g, 0, 0)),
-            whole(rows), whole(WIDE), whole(rows), whole(WIDE),
+            whole, whole, whole, whole,
         ],
         out_specs=[
             pl.BlockSpec((1, rows, WIDE), lambda g: (0, 0, g)),
@@ -118,8 +140,8 @@
         name="own_part",
     )(
         mom, grad, pos,
-        basis_parts(nx, False), basis_parts(blocks, True),
-        basis_parts(nx, True), basis_parts(blocks, False),
+        left_basis(basis()), right_basis(basis().T),
+        left_basis(basis().T), right_basis(basis()),
     )
 
 
@@ -182,50 +204,104 @@
     )(mine)
 
 
-def sum_kernel(nx, topk, reps, _, data, weight, li, ri, smooth_out, weight_out):
-    rows, cols = down(GROUP), down(WIDE)
-    tiles = []
+def regroup(tiles, topk):
+    lane = lax.broadcasted_iota(jnp.int32, tiles[0].shape, 1) // topk
+    each = LANES // topk
+    out = []
+    for y in range(each):
+        mixed = tiles[y]
+        for j in range(each):
+            if j != y:
+                moved = pltpu.roll(tiles[j], (j - y) % each * topk, axis=1)
+                mixed = jnp.where(lane == j, moved, mixed)
+        out.append(mixed)
+    return out
+
+
+def scatter(nx, topk, tiles):
+    each = LANES // topk
+    rows = down(GROUP)
+    fields = [[] for _ in range(each)]
+    for q in range(0, len(tiles), each):
+        for y, tile in enumerate(regroup(tiles[q : q + each], topk)):
+            a = jnp.floor(tile * (1.0 / GROUP))
+            high, low = split(tile)
+            fields[y].append((a, tile - a * GROUP, high.astype(f32), low.astype(f32)))
+    grid = []
     for x in range(nx):
-        lefts, rights = [], []
-        for r in range(reps):
-            tile = data[0, r, 0]
-            a, b = place(tile[nx + x : nx + x + 1], topk)
-            high, low = split(tile[x : x + 1])
-            at_row = rows == a
-            lefts.append(jnp.concatenate([
-                jnp.where(at_row, high.astype(f32), 0.0).astype(bf16),
-                jnp.where(at_row, low.astype(f32), 0.0).astype(bf16),
-            ], axis=0))
-            rights.append(jnp.where(cols == b, 1.0, 0.0).astype(bf16))
-        both = dot_t(jnp.concatenate(lefts, axis=1), jnp.concatenate(rights, axis=1))
-        tiles.append(both[:GROUP] + both[GROUP:])
-    smooth = jnp.tanh(right(left(li, jnp.concatenate(tiles, axis=0)), ri))
-    smooth_out[...] = smooth.astype(bf16)
-    weight_out[...] = (weight[...].astype(f32) - step_rate * smooth).astype(bf16)
+        across = []
+        for y in range(each):
+            ones, values = [], []
+            for a, b, high, low in fields[y]:
+                at_a = rows == a[nx + x : nx + x + 1]
+                at_b = rows == b[nx + x : nx + x + 1]
+                plain, scaled = (at_a, at_b) if y % 2 == 0 else (at_b, at_a)
+                ones.append(jnp.where(plain, 1.0, 0.0).astype(bf16))
+                values.append(jnp.concatenate([
+                    jnp.where(scaled, high[x : x + 1], 0.0).astype(bf16),
+                    jnp.where(scaled, low[x : x + 1], 0.0).astype(bf16),
+                ], axis=0))
+            ones, values = jnp.concatenate(ones, axis=1), jnp.concatenate(values, axis=1)
+            if y % 2 == 0:
+                both = dot_t(ones, values)
+                across.append((both + pltpu.roll(both, GROUP, axis=1))[:, :GROUP])
+            else:
+                both = dot_t(values, ones)
+                across.append(both[:GROUP] + both[GROUP:])
+        grid.append(jnp.concatenate(across, axis=1))
+    return jnp.concatenate(grid, axis=0)
+
+
+def sum_kernel(nx, topk, reps, _, data, weight, li, ri, smooth_out, weight_out, sums):
+    g, last = pl.program_id(0), pl.num_programs(0) - 1
+
+    def gather():
+        sums[lax.rem(g, 2)] = scatter(nx, topk, [data[0, r, 0] for r in range(reps)])
+
+    def finish():
+        smooth = jnp.tanh(right(left(li[...], sums[lax.rem(g + 1, 2)]), ri[...]))
+        smooth_out[...] = smooth.astype(bf16)
+        weight_out[...] = (weight[...].astype(f32) - step_rate * smooth).astype(bf16)
+
+    @pl.when(g == 0)
+    def _():
+        gather()
+
+    @pl.when((g > 0) & (g < last))
+    def _():
+        finish()
+        gather()
+
+    @pl.when(g == last)
+    def _():
+        finish()
 
 
 def sum_part(shard, data, weight, topk, interpret=False):
     rows, width = weight.shape
     nx = rows // GROUP
     reps = data.shape[1]
-    blocks = WIDE // GROUP
-    column = pl.BlockSpec((rows, WIDE), lambda g, s: (0, g))
-    whole = lambda n: pl.BlockSpec((2, n, n), lambda g, s: (0, 0, 0))
+    steps = width // WIDE
+    column = pl.BlockSpec((rows, WIDE), lambda g, s: (0, jnp.maximum(g - 1, 0)))
+    whole = pl.BlockSpec((2 * PAIR, 2 * PAIR), lambda g, s: (0, 0))
     return pl.pallas_call(
         functools.partial(sum_kernel, nx, topk, reps),
         grid_spec=pltpu.PrefetchScalarGridSpec(
             num_scalar_prefetch=1,
-            grid=(width // WIDE,),
+            grid=(steps + 1,),
             in_specs=[
-                pl.BlockSpec((1, reps, 1, 2 * nx, LANES), lambda g, s: (s[0], 0, g, 0, 0)),
-                column, whole(rows), whole(WIDE),
+                pl.BlockSpec(
+                    (1, reps, 1, 2 * nx, LANES), lambda g, s: (s[0], 0, jnp.minimum(g, steps - 1), 0, 0)
+                ),
+                column, whole, whole,
             ],
             out_specs=[column, column],
+            scratch_shapes=[pltpu.VMEM((2, rows, WIDE), f32)],
         ),
         out_shape=[jax.ShapeDtypeStruct((rows, width), bf16)] * 2,
         interpret=interpret,
         name="sum_part",
-    )(shard, data, weight, basis_parts(nx, True), basis_parts(blocks, False))
+    )(shard, data, weight, left_basis(basis().T), right_basis(basis()))
 
 
 def per_device(reps, shards, weight, momentum, grad, positions):

time: 107 us -> 88.3 us (0.83)
  Pallas kernels: 94.5 us -> 75.3 us
    pallas_call x2, Pallas kernels: 38.3 us -> 21.7 us  [sum_part(): pl.pallas_call(functools.partial(sum_kernel, nx, topk, reps), grid_spec=p...]
    pallas_call x1, Pallas kernels: 21.9 us -> 19.3 us  [own_part(): pl.pallas_call(functools.partial(own_kernel, nx, topk), grid=(steps,), in...]
  transfers between devices with their start and end apart: 4 -> 4, of which waited for: 0 -> 0; matrix products, arithmetic and copies ran while one was open for 5% -> 6% of each run, Pallas kernels for 89% -> 86%
where the time goes in v1:
time: 88.3 us; the launch traced here: 87.5 us
  Pallas kernels  75.3 us (85%)
  other arithmetic  8.03 us (9%)
  local copies, waits for them, and re-layouts  2.47 us (3%)
  starting transfers between devices  0.95 us (1%)
    pallas_call x1, Pallas kernels, swap(): pl.pallas_call(functools.partial(swap_kernel, reps, shards), in_specs=[pl...  34.3 us
    pallas_call x2, Pallas kernels, sum_part(): pl.pallas_call(functools.partial(sum_kernel, nx, topk, reps), grid_spec=p...  21.7 us
    pallas_call x1, Pallas kernels, own_part(): pl.pallas_call(functools.partial(own_kernel, nx, topk), grid=(steps,), in...  19.3 us
    select_n x2, other arithmetic, per_device(): jnp.where(core == 0, a, b)  3.38 us
    concatenate x1, other arithmetic, per_device(): return (kept, direction, jnp.concatenate(columns, axis=1))  2.23 us
  transfers between devices with their start and end apart: 4, of which 0 were waited for; matrix products, arithmetic and copies ran while one was open for 6% of the time, Pallas kernels for 86%

profile of v1, /device:TPU:15, one launch (start us, length us, event | category | flops | bytes accessed | tf_op | source)
XLA Modules:
  0.0 87.5 jit_solution(11068866857892006380)
XLA Ops:
  0.6 0.0 copy-start
  0.7 1.6 %copy-done = bf16[256,4096]{1,0:T(8,128)(2,1)S(1)} copy-done((bf16[256,4096]{1,0:T(8,128)(2,1)S(1)}, bf16[256,4096]{1,0:T(8,128)(2,1)}, u32[]{:S(2)}) %copy-start) | copy-done | bytes 2097176
  2.2 0.1 constant_dynamic-slice_fusion.weight
  2.3 0.0 copy-start.1
  2.3 0.3 collective-permute-start.1
  2.6 0.9 %convert_element_type.7 = f32[1,4,64,32]{2,3,1,0:T(8,128)S(1)} convert(s32[1,4,64,32]{2,3,1,0:T(8,128)} %param.15) | non-fusion elementwise | flops 8192 | bytes 65536 | tf_op jit(solution)/shard_map/convert_element_type | solution.py:321
  3.5 0.1 copy.15
  3.6 0.1 convert_element_type.8
  3.7 0.6 copy.18
  4.3 19.3 %own_part.1 = (f32[1,256,4096]{2,1,0:T(8,128)}, f32[16,8,128]{2,1,0:T(8,128)}) custom-call(f32[1,256,4096]{2,1,0:T(8,128)} %mom.1, bf16[1,256,4096]{2,1,0:T(8,128)(2,1)} %grad.1, f32[16,4,128]{2,1,0:T(4,128)} %bitcast.8, bf16[256,256]{1,0:T(8,128)(2,1)} %constant.34.clone.lf, bf16[256,256]{1,0:T(8,128)(2,1)} %constant.35.clone.rt, ...), custom_call_target="tpu_custom_call" | custom-call | tf_op jit(solution)/shard_map/own_part/pallas_call | solution.py:122
  23.6 34.3 %swap.1.data = f32[2,16,8,8,128]{4,3,2,1,0:T(8,128)} custom-call(f32[2,8,8,128]{3,2,1,0:T(8,128)} %bitcast.9), custom_call_target="tpu_custom_call" | custom-call | tf_op jit(solution)/shard_map/swap/pallas_call | solution.py:192
  58.0 0.0 copy-done.1
  58.0 10.8 %sum_part.2 = (bf16[256,2048]{1,0:T(8,128)(2,1)}, bf16[256,2048]{1,0:T(8,128)(2,1)}) custom-call(s32[1]{0:T(128)} %bitcast.1._, f32[2,16,8,8,128]{4,3,2,1,0:T(8,128)} %swap.1.data, bf16[256,2048]{1,0:T(8,128)(2,1)} %copy-done.1, bf16[256,256]{1,0:T(8,128)(2,1)} %constant.36.clone.li, bf16[256,256]{1,0:T(8,128)(2,1)} %constant.37.clone.ri), custom_call_target="tpu_custom_call" | custom-call | tf_op jit(solution)/shard_map/sum_part/pallas_call | solution.py:287
  68.9 0.0 collective-permute-start
  68.9 0.5 collective-permute-start.3
  69.4 0.0 collective-permute-done.1.weight
  69.4 10.8 %sum_part.3 = (bf16[256,2048]{1,0:T(8,128)(2,1)}, bf16[256,2048]{1,0:T(8,128)(2,1)}) custom-call(s32[1]{0:T(128)} %bitcast.3._, f32[2,16,8,8,128]{4,3,2,1,0:T(8,128)} %swap.1.data, bf16[256,2048]{1,0:T(8,128)(2,1)} %collective-permute-done.1.weight, bf16[256,256]{1,0:T(8,128)(2,1)} %constant.36.clone.li, bf16[256,256]{1,0:T(8,128)(2,1)} %constant.37.clone.ri), custom_call_target="tpu_custom_call" | custom-call | tf_op jit(solution)/shard_map/sum_part/pallas_call | solution.py:287
  80.2 0.0 copy-start.2
  80.2 0.0 copy-start.3
  80.2 0.1 collective-permute-start.2
  80.3 0.0 collective-permute-done
  80.3 1.8 %broadcast_select_fusion.9 = (bf16[256,2048]{1,0:T(8,128)(2,1)S(1)}, bf16[256,2048]{1,0:T(8,128)(2,1)S(1)}) fusion(bf16[256,2048]{1,0:T(8,128)(2,1)} %get-tuple-element.10, bf16[256,2048]{1,0:T(8,128)(2,1)} %collective-permute-done, pred[]{:T(512)S(6)} %eq.6), kind=kLoop, calls=%fused_computation.11 | loop fusion | flops 1048576 | bytes 4194305 | tf_op jit(solution)/shard_map/jit(_where)/select_n | solution.py:327
  82.1 1.5 %pad_maximum_fusion.1 = bf16[256,4096]{1,0:T(8,128)(2,1)} fusion(bf16[256,2048]{1,0:T(8,128)(2,1)S(1)} %get-tuple-element.18, bf16[256,2048]{1,0:T(8,128)(2,1)S(1)} %get-tuple-element.17), kind=kLoop, calls=%fused_computation.1 | loop fusion | flops 4194304 | bytes 4194304 | tf_op jit(solution)/shard_map/concatenate | solution.py:333
  83.7 0.0 collective-permute-done.3
  83.7 0.0 collective-permute-done.2
  83.7 0.0 copy-done.2
  83.7 0.0 copy-done.3
  83.7 1.6 %broadcast_select_fusion.7 = (bf16[256,2048]{1,0:T(8,128)(2,1)S(1)}, bf16[256,2048]{1,0:T(8,128)(2,1)S(1)}, bf16[256,2048]{1,0:T(8,128)(2,1)S(1)}, bf16[256,2048]{1,0:T(8,128)(2,1)S(1)}) fusion(pred[]{:T(512)S(6)} %eq.6, bf16[256,2048]{1,0:T(8,128)(2,1)S(1)} %copy-done.3, bf16[256,2048]{1,0:T(8,128)(2,1)S(1)} %copy-done.2, pred[]{:T(512)S(6)} %eq.7, ...), kind=kLoop, calls=%fused_computation.9 | loop fusion | flops 4194304 | bytes 8388611 | tf_op jit(solution)/shard_map/jit(_where)/select_n | solution.py:327
  85.3 2.2 %pad_maximum_fusion = bf16[256,8192]{1,0:T(8,128)(2,1)} fusion(bf16[256,2048]{1,0:T(8,128)(2,1)S(1)} %get-tuple-element.16, bf16[256,2048]{1,0:T(8,128)(2,1)S(1)} %get-tuple-element.15, bf16[256,2048]{1,0:T(8,128)(2,1)S(1)} %get-tuple-element.14, bf16[256,2048]{1,0:T(8,128)(2,1)S(1)} %get-tuple-element.13), kind=kLoop, calls=%fused_computation | loop fusion | flops 16777216 | bytes 8388608 | tf_op jit(solution)/shard_map/concatenate | solution.py:344
Async XLA Ops:
  0.6 1.6 %copy-start = (bf16[256,4096]{1,0:T(8,128)(2,1)S(1)}, bf16[256,4096]{1,0:T(8,128)(2,1)}, u32[]{:S(2)}) copy-start(bf16[256,4096]{1,0:T(8,128)(2,1)} %param.12) | copy-start | bytes 6291460
  2.3 55.7 %copy-start.1 = (bf16[256,2048]{1,0:T(8,128)(2,1)}, bf16[256,2048]{1,0:T(8,128)(2,1)S(1)}, u32[]{:S(2)}) copy-start(bf16[256,2048]{1,0:T(8,128)(2,1)S(1)} %constant_dynamic-slice_fusion.weight) | copy-start | bytes 3145732
  2.3 67.1 %collective-permute-start.1 = (bf16[256,2048]{1,0:T(8,128)(2,1)S(1)}, bf16[256,2048]{1,0:T(8,128)(2,1)}, u32[]{:S(2)}, u32[]{:S(2)}) collective-permute-start(bf16[256,2048]{1,0:T(8,128)(2,1)S(1)} %constant_dynamic-slice_fusion.weight), channel_id=1, source_target_pairs={{0,1},{1,0},{2,3},{3,2},{4,5},{5,4},{6,7},{7,6},{8,9},{9,8},{10,11... | collective-permute-start | bytes 3145736 | tf_op jit(solution)/shard_map/ppermute | solution.py:317
  68.9 11.5 %collective-permute-start = (bf16[256,2048]{1,0:T(8,128)(2,1)}, bf16[256,2048]{1,0:T(8,128)(2,1)}, u32[]{:S(2)}, u32[]{:S(2)}) collective-permute-start(bf16[256,2048]{1,0:T(8,128)(2,1)} %get-tuple-element.10), channel_id=1, source_target_pairs={{0,2},{2,0},{4,6},{6,4},{8,10},{10,8},{12,14},{14,12},{16,18},{18,... | collective-permute-start | bytes 3145736 | tf_op jit(solution)/shard_map/ppermute | solution.py:326
  68.9 14.8 %collective-permute-start.3 = (bf16[256,2048]{1,0:T(8,128)(2,1)}, bf16[256,2048]{1,0:T(8,128)(2,1)}, u32[]{:S(2)}, u32[]{:S(2)}) collective-permute-start(bf16[256,2048]{1,0:T(8,128)(2,1)} %get-tuple-element.12), channel_id=1, source_target_pairs={{0,2},{2,0},{4,6},{6,4},{8,10},{10,8},{12,14},{14,12},{16,18},{18,... | collective-permute-start | bytes 3145736 | tf_op jit(solution)/shard_map/ppermute | solution.py:326
  80.2 3.5 %copy-start.2 = (bf16[256,2048]{1,0:T(8,128)(2,1)S(1)}, bf16[256,2048]{1,0:T(8,128)(2,1)}, u32[]{:S(2)}) copy-start(bf16[256,2048]{1,0:T(8,128)(2,1)} %get-tuple-element.12) | copy-start | bytes 3145732
  80.2 3.5 %copy-start.3 = (bf16[256,2048]{1,0:T(8,128)(2,1)S(1)}, bf16[256,2048]{1,0:T(8,128)(2,1)}, u32[]{:S(2)}) copy-start(bf16[256,2048]{1,0:T(8,128)(2,1)} %get-tuple-element.11) | copy-start | bytes 3145732
  80.2 3.5 %collective-permute-start.2 = (bf16[256,2048]{1,0:T(8,128)(2,1)}, bf16[256,2048]{1,0:T(8,128)(2,1)S(1)}, u32[]{:S(2)}, u32[]{:S(2)}) collective-permute-start(bf16[256,2048]{1,0:T(8,128)(2,1)} %get-tuple-element.11), channel_id=1, source_target_pairs={{0,2},{2,0},{4,6},{6,4},{8,10},{10,8},{12,14},{14,12},{16,18},{18,... | collective-permute-start | bytes 3145736 | tf_op jit(solution)/shard_map/ppermute | solution.py:326

commit v2 on v1

v2 whole, which is shorter than its diff:
```python
import functools
import math

import jax
import jax.numpy as jnp
import numpy as np
from jax import lax
from jax.experimental import pallas as pl
from jax.experimental.pallas import tpu as pltpu
from jax.sharding import PartitionSpec as P

GROUP = 64
LANES = 128
WIDE = 256
PAIR = 128
CHUNKS = 2

beta_decay = 0.9
step_rate = 0.02

f32, bf16 = jnp.float32, jnp.bfloat16
MESH = pl.DeviceIdType.MESH


def basis():
    k = np.arange(GROUP, dtype=np.float64)[:, None]
    i = np.arange(GROUP, dtype=np.float64)[None, :]
    scale = np.where(k == 0, math.sqrt(1.0 / GROUP), math.sqrt(2.0 / GROUP))
    return scale * np.cos(math.pi * (2.0 * i + 1.0) * k / (2.0 * GROUP))


def halves(c):
    full = np.kron(np.eye(PAIR // GROUP), c).astype(np.float32)
    high = full.astype(bf16)
    low = (full - high.astype(np.float32)).astype(bf16)
    return high, low


def left_basis(c):
    high, low = halves(c)
    return np.block([[high, high], [low, low]])


def right_basis(c):
    high, low = halves(c)
    return np.block([[high, low], [high, low]])


def split(x):
    high = x.astype(bf16)
    return high, (x - high.astype(f32)).astype(bf16)


def dot(a, b):
    return jnp.dot(a, b, preferred_element_type=f32)


def dot_t(a, b):
    return lax.dot_general(a, b, (((1,), (1,)), ((), ())), preferred_element_type=f32)


def left(m, x):
    high, low = split(x)
    parts = []
    for at in range(0, x.shape[0], PAIR):
        both = dot(m, jnp.concatenate([high[at : at + PAIR], low[at : at + PAIR]], axis=0))
        parts.append(both[:PAIR] + both[PAIR:])
    return jnp.concatenate(parts, axis=0)


def right(x, m):
    high, low = split(x)
    rows = x.shape[0]
    ats = range(0, x.shape[1], PAIR)
    both = dot(jnp.concatenate([
        jnp.concatenate([high[:, at : at + PAIR], low[:, at : at + PAIR]], axis=1) for at in ats
    ], axis=0), m)
    both = both[:, :PAIR] + both[:, PAIR:]
    return jnp.concatenate([both[i * rows : (i + 1) * rows] for i in range(len(ats))], axis=1)


def down(rows):
    return lax.broadcasted_iota(jnp.int32, (rows, LANES), 0).astype(f32)


def lane_offset(topk):
    lane = lax.broadcasted_iota(jnp.int32, (1, LANES), 1)
    return (lane // topk * GROUP).astype(f32)


def place(pos, topk):
    a = jnp.floor(pos * (1.0 / GROUP))
    return a, pos - a * GROUP + lane_offset(topk)


def own_kernel(nx, topk, reps, shards, mom, grad, pos, places, lf, rt, li, ri, kept, vals, spots, mine, *sems):
    g, steps = pl.program_id(0), pl.num_programs(0)
    lf, rt, li, ri = lf[...], rt[...], li[...], ri[...]
    tiles = mine.shape[1]
    chunk = tiles // CHUNKS
    period = 2 * chunk
    r, s = lax.axis_index("replica"), lax.axis_index("shard")
    me = r * shards + s
    total = reps * shards
    place_send, place_recv, place_own, send_sem, recv_sem, own_sem = sems

    def peer(step):
        to = lax.rem(me + step, total)
        return to // shards, lax.rem(to, shards)

    def place_copy(step):
        to_r, to_s = peer(step)
        return pltpu.make_async_remote_copy(
            src_ref=places.at[lax.rem(to_r, 2)], dst_ref=spots.at[s, r],
            send_sem=place_send.at[step], recv_sem=place_recv.at[step],
            device_id=(to_r, to_s), device_id_type=MESH,
        )

    def value_copy(step, half, c):
        to_r, to_s = peer(step)
        part = pl.ds(c * chunk, chunk)
        return pltpu.make_async_remote_copy(
            src_ref=mine.at[half, part], dst_ref=vals.at[s, r, part],
            send_sem=send_sem.at[c, step], recv_sem=recv_sem.at[c, step],
            device_id=(to_r, to_s), device_id_type=MESH,
        )

    def place_keep():
        return pltpu.make_async_copy(places.at[lax.rem(r, 2)], spots.at[s, r], place_own)

    def value_keep(half, c):
        part = pl.ds(c * chunk, chunk)
        return pltpu.make_async_copy(mine.at[half, part], vals.at[s, r, part], own_sem.at[c])

    @pl.when(g == 0)
    def _():
        place_keep().start()

        @pl.loop(1, total)
        def _(step):
            place_copy(step).start()

    moved = beta_decay * mom[0] + grad[0].astype(f32)
    coeff = right(left(lf, moved), rt)
    at = pos[0]
    a, b = place(at, topk)
    rows, cols = down(GROUP), down(WIDE)
    picked, own = [], []
    for x in range(nx):
        part = coeff[x * GROUP : (x + 1) * GROUP]
        at_row = rows == a[x : x + 1]
        hot_a = jnp.where(at_row, 1.0, 0.0).astype(bf16)
        hot_b = jnp.where(cols == b[x : x + 1], 1.0, 0.0).astype(bf16)
        own.append(part * dot_t(hot_a, hot_b))
        high, low = split(part)
        found = dot(jnp.concatenate([high, low], axis=0), hot_b)
        found = found[:GROUP] + found[GROUP:]
        picked.append(jnp.sum(jnp.where(at_row, found, 0.0), axis=0, keepdims=True))
    kept[0] = moved - right(left(li, jnp.concatenate(own, axis=0)), ri)
    picked = jnp.concatenate(picked, axis=0)
    half_of, tile_of = g // (2 * tiles), lax.rem(g // 2, tiles)
    mine[half_of, tile_of, pl.ds(pl.multiple_of(lax.rem(g, 2) * nx, nx), nx)] = picked

    for half in range(2):
        for c in range(CHUNKS):
            @pl.when(g == half * 2 * tiles + (c + 1) * period - 1)
            def _(half=half, c=c):
                @pl.loop(1, total)
                def _(step):
                    @pl.when(lax.rem(peer(step)[0], 2) == half)
                    def _():
                        value_copy(step, half, c).start()

                @pl.when(lax.rem(r, 2) == half)
                def _():
                    value_keep(half, c).start()

    @pl.when(g == steps - 1)
    def _():
        place_keep().wait()
        for c in range(CHUNKS):
            value_keep(0, c).wait()

        @pl.loop(1, total)
        def _(step):
            of = lax.rem(me - step + total, total)
            of_r, of_s = of // shards, lax.rem(of, shards)
            copy = place_copy(step)
            copy.wait_send()
            pltpu.make_async_remote_copy(
                src_ref=places.at[0], dst_ref=spots.at[of_s, of_r],
                send_sem=place_send.at[step], recv_sem=place_recv.at[step],
                device_id=(of_r, of_s), device_id_type=MESH,
            ).wait_recv()
            for c in range(CHUNKS):
                part = pl.ds(c * chunk, chunk)
                value_copy(step, 0, c).wait_send()
                pltpu.make_async_remote_copy(
                    src_ref=mine.at[0, part], dst_ref=vals.at[of_s, of_r, part],
                    send_sem=send_sem.at[c, step], recv_sem=recv_sem.at[c, step],
                    device_id=(of_r, of_s), device_id_type=MESH,
                ).wait_recv()


def own_part(mom, grad, pos, places, reps, shards, topk):
    _, rows, width = mom.shape
    nx = rows // GROUP
    steps = width // WIDE
    tiles = steps // 4
    total = reps * shards
    whole = pl.BlockSpec((2 * PAIR, 2 * PAIR), lambda g: (0, 0))
    dma = pltpu.SemaphoreType.DMA
    return pl.pallas_call(
        functools.partial(own_kernel, nx, topk, reps, shards),
        grid=(steps,),
        in_specs=[
            pl.BlockSpec((1, rows, WIDE), lambda g: (0, 0, g)),
            pl.BlockSpec((1, rows, WIDE), lambda g: (0, 0, g)),
            pl.BlockSpec((1, nx, LANES), lambda g: (g, 0, 0)),
            pl.BlockSpec(memory_space=pl.ANY),
            whole, whole, whole, whole,
        ],
        out_specs=[
            pl.BlockSpec((1, rows, WIDE), lambda g: (0, 0, g)),
            pl.BlockSpec(memory_space=pl.ANY),
            pl.BlockSpec(memory_space=pl.ANY),
        ],
        out_shape=[
            jax.ShapeDtypeStruct((1, rows, width), f32),
            jax.ShapeDtypeStruct((shards, reps, tiles, 2 * nx, LANES), f32),
            jax.ShapeDtypeStruct((shards, reps) + places.shape[1:], jnp.int16),
        ],
        scratch_shapes=[
            pltpu.VMEM((2, tiles, 2 * nx, LANES), f32),
            dma((total,)), dma((total,)), dma,
            dma((CHUNKS, total)), dma((CHUNKS, total)), dma((CHUNKS,)),
        ],
        compiler_params=pltpu.CompilerParams(has_side_effects=True),
        name="own_part",
    )(
        mom, grad, pos, places,
        left_basis(basis()), right_basis(basis().T),
        left_basis(basis().T), right_basis(basis()),
    )


def regroup(tiles, topk):
    lane = lax.broadcasted_iota(jnp.int32, tiles[0].shape, 1) // topk
    each = LANES // topk
    out = []
    for y in range(each):
        mixed = tiles[y]
        for j in range(each):
            if j != y:
                moved = pltpu.roll(tiles[j], (j - y) % each * topk, axis=1)
                mixed = jnp.where(lane == j, moved, mixed)
        out.append(mixed)
    return out


def scatter(nx, topk, values, spots):
    each = LANES // topk
    rows = down(GROUP)
    fields = [[] for _ in range(each)]
    for q in range(0, len(values), each):
        mixed = zip(regroup(values[q : q + each], topk), regroup(spots[q : q + each], topk))
        for y, (value, spot) in enumerate(mixed):
            a = jnp.floor(spot * (1.0 / GROUP))
            high, low = split(value)
            fields[y].append((a, spot - a * GROUP, high.astype(f32), low.astype(f32)))
    grid = []
    for x in range(nx):
        across = []
        for y in range(each):
            ones, scaled = [], []
            for a, b, high, low in fields[y]:
                at_a = rows == a[x : x + 1]
                at_b = rows == b[x : x + 1]
                plain, chosen = (at_a, at_b) if y % 2 == 0 else (at_b, at_a)
                ones.append(jnp.where(plain, 1.0, 0.0).astype(bf16))
                scaled.append(jnp.concatenate([
                    jnp.where(chosen, high[x : x + 1], 0.0).astype(bf16),
                    jnp.where(chosen, low[x : x + 1], 0.0).astype(bf16),
                ], axis=0))
            ones, scaled = jnp.concatenate(ones, axis=1), jnp.concatenate(scaled, axis=1)
            if y % 2 == 0:
                both = dot_t(ones, scaled)
                across.append((both + pltpu.roll(both, GROUP, axis=1))[:, :GROUP])
            else:
                both = dot_t(scaled, ones)
                across.append(both[:GROUP] + both[GROUP:])
        grid.append(jnp.concatenate(across, axis=1))
    return jnp.concatenate(grid, axis=0)


def sum_kernel(nx, topk, reps, _, vals, spots, weight, li, ri, smooth_out, weight_out, sums, at):
    g, last = pl.program_id(0), pl.num_programs(0) - 1

    def gather():
        rows = pl.ds(pl.multiple_of(lax.rem(g, 2) * nx, nx), nx)
        tile = g // 2
        sums[lax.rem(g, 2)] = scatter(
            nx, topk, [vals[0, r, 0, rows] for r in range(reps)], [at[r, tile, rows] for r in range(reps)]
        )

    def finish():
        smooth = jnp.tanh(right(left(li[...], sums[lax.rem(g + 1, 2)]), ri[...]))
        smooth_out[...] = smooth.astype(bf16)
        weight_out[...] = (weight[...].astype(f32) - step_rate * smooth).astype(bf16)

    @pl.when(g == 0)
    def _():
        for r in range(reps):
            at[r] = spots[0, r].astype(jnp.int32).astype(f32).reshape(at.shape[1:])
        gather()

    @pl.when((g > 0) & (g < last))
    def _():
        finish()
        gather()

    @pl.when(g == last)
    def _():
        finish()


def sum_part(shard, vals, spots, weight, topk):
    rows, width = weight.shape
    nx = rows // GROUP
    reps, tiles = vals.shape[1:3]
    steps = width // WIDE
    column = pl.BlockSpec((rows, WIDE), lambda g, s: (0, jnp.maximum(g - 1, 0)))
    whole = pl.BlockSpec((2 * PAIR, 2 * PAIR), lambda g, s: (0, 0))
    return pl.pallas_call(
        functools.partial(sum_kernel, nx, topk, reps),
        grid_spec=pltpu.PrefetchScalarGridSpec(
            num_scalar_prefetch=1,
            grid=(steps + 1,),
            in_specs=[
                pl.BlockSpec(
                    (1, reps, 1, 2 * nx, LANES),
                    lambda g, s: (s[0], 0, jnp.minimum(g, steps - 1) // 2, 0, 0),
                ),
                pl.BlockSpec((1,) + spots.shape[1:], lambda g, s: (s[0], 0, 0, 0)),
                column, whole, whole,
            ],
            out_specs=[column, column],
            scratch_shapes=[
                pltpu.VMEM((2, rows, WIDE), f32), pltpu.VMEM((reps, tiles, 2 * nx, LANES), f32),
            ],
        ),
        out_shape=[jax.ShapeDtypeStruct((rows, width), bf16)] * 2,
        name="sum_part",
    )(shard, vals, spots, weight, left_basis(basis().T), right_basis(basis()))


def per_device(reps, shards, weight, momentum, grad, positions):
    rows, width = weight.shape
    _, nx, ny, topk = positions.shape
    half = width // 2
    steps = width // WIDE
    r, s = lax.axis_index("replica"), lax.axis_index("shard")
    core = lax.rem(r, 2)

    mine_w = lax.dynamic_slice(weight, (0, core * half), (rows, half))
    weights = [mine_w] + [
        lax.ppermute(mine_w, "shard", [(i, (i + d) % shards) for i in range(shards)])
        for d in range(1, shards)
    ]

    pos = positions[0].reshape(nx, steps, LANES).transpose(1, 0, 2)
    places = pos.astype(jnp.int16).reshape(2, steps // 2 * nx, LANES)
    kept, vals, spots = own_part(momentum, grad, pos.astype(f32), places, reps, shards, topk)

    pairs = [(i, i ^ 1) for i in range(reps)]
    flip = lambda x: lax.ppermute(x, "replica", pairs)
    order = lambda a, b: [jnp.where(core == 0, a, b), jnp.where(core == 0, b, a)]
    pieces, direction = [], None
    for d in range(shards):
        of = lax.rem(s - d + shards, shards)
        smooth, updated = sum_part(of.reshape(1).astype(jnp.int32), vals, spots, weights[d], topk)
        if d == 0:
            direction = jnp.concatenate(order(smooth, flip(smooth)), axis=1)
        pieces.append((updated, flip(updated)))

    columns = []
    for t in range(shards):
        d = lax.rem(s - t + shards, shards)
        a, b = pieces[0]
        for e in range(1, shards):
            a = jnp.where(d == e, pieces[e][0], a)
            b = jnp.where(d == e, pieces[e][1], b)
        columns += order(a, b)
    return (kept, direction, jnp.concatenate(columns, axis=1))


def solution(mesh):
    reps, shards = mesh.shape["replica"], mesh.shape["shard"]
    in_specs = (
        P(None, "shard"),
        P("replica", None, "shard"),
        P("replica", None, "shard"),
        P("replica", None, "shard", None),
    )
    out_specs = (P("replica", None, "shard"), P(None, "shard"), P())
    return jax.shard_map(
        functools.partial(per_device, reps, shards),
        mesh=mesh, in_specs=in_specs, out_specs=out_specs, check_vma=False,
    )
```

time: 88.3 us -> 79.6 us (0.901)
  the two profiles are of different devices: /device:TPU:15 before, /device:TPU:0 now
where the time goes in v2:
time: 79.6 us; the launch traced here: 79.1 us
  Pallas kernels  55.2 us (69%)
  starting transfers between devices  8.32 us (10%)
  other arithmetic  8.17 us (10%)
  local copies, waits for them, and re-layouts  6.67 us (8%)
    pallas_call x1, Pallas kernels, own_part(): pl.pallas_call(functools.partial(own_kernel, nx, topk, reps, shards), gri...  33 us
    pallas_call x2, Pallas kernels, sum_part(): pl.pallas_call(functools.partial(sum_kernel, nx, topk, reps), grid_spec=p...  22.1 us
    ppermute x3, starting transfers between devices, per_device(): flip = lambda x: lax.ppermute(x, 'replica', pairs)  5.29 us
    unnamed x11, local copies, waits for them, and re-layouts  4.95 us
    select_n x2, other arithmetic, per_device(): jnp.where(core == 0, a, b)  3.35 us
    ppermute x1, starting transfers between devices, per_device(): lax.ppermute(mine_w, 'shard', [(i, (i + d) % shards) for i in range(shard...  3.03 us
    concatenate x1, other arithmetic, per_device(): return (kept, direction, jnp.concatenate(columns, axis=1))  2.35 us
  transfers between devices with their start and end apart: 4, of which 0 were waited for; matrix products, arithmetic and copies ran while one was open for 7% of the time, Pallas kernels for 70%

profile of v2, /device:TPU:0, one launch (start us, length us, event | category | flops | bytes accessed | tf_op | source)
XLA Modules:
  0.0 79.1 jit_solution(7966104810560437919)
XLA Ops:
  0.6 0.0 copy-start
  0.7 1.6 %copy-done = bf16[256,4096]{1,0:T(8,128)(2,1)S(1)} copy-done((bf16[256,4096]{1,0:T(8,128)(2,1)S(1)}, bf16[256,4096]{1,0:T(8,128)(2,1)}, u32[]{:S(2)}) %copy-start) | copy-done | bytes 2097176
  2.2 0.1 constant_dynamic-slice_fusion.weight
  2.3 0.0 copy-start.1
  2.3 3.0 %collective-permute-start.1 = (bf16[256,2048]{1,0:T(8,128)(2,1)S(1)}, bf16[256,2048]{1,0:T(8,128)(2,1)}, u32[]{:S(2)}, u32[]{:S(2)}) collective-permute-start(bf16[256,2048]{1,0:T(8,128)(2,1)S(1)} %constant_dynamic-slice_fusion.weight), channel_id=1, source_target_pairs={{0,1},{1,0},{2,3},{3,2},{4,5},{5,4},{6,7},{7,6},{8,9},{9,8},{10,11... | collective-permute-start | bytes 3145736 | tf_op jit(solution)/shard_map/ppermute | solution.py:367
  5.3 0.9 %fusion = (s16[1,4,64,32]{2,3,1,0:T(8,128)(2,1)S(1)}, f32[1,4,64,32]{2,3,1,0:T(8,128)S(1)}) fusion(s32[1,4,64,32]{2,3,1,0:T(8,128)} %param.15), kind=kLoop, calls=%fused_computation.14 | loop fusion | flops 16384 | bytes 81920 | tf_op jit(solution)/shard_map/convert_element_type | solution.py:372
  6.3 0.1 copy.15
  6.4 0.1 convert_element_type.17
  6.5 0.6 copy.20
  7.1 0.1 copy.17
  7.2 0.1 convert_element_type.20
  7.3 0.6 copy.18
  8.0 33.0 %own_part.1 = (f32[1,256,4096]{2,1,0:T(8,128)}, f32[2,16,4,8,128]{4,3,2,1,0:T(8,128)}, s16[2,16,32,128]{3,2,1,0:T(8,128)(2,1)}) custom-call(f32[1,256,4096]{2,1,0:T(8,128)} %mom.1, bf16[1,256,4096]{2,1,0:T(8,128)(2,1)} %grad.1, f32[16,4,128]{2,1,0:T(4,128)} %bitcast.11, s16[2,32,128]{2,1,0:T(8,128)(2,1)} %bitcast.12, bf16[256,256]{1,0:T(8,128)(2,1)} %constant.34.clone.lf, ...), custom_call_target="tpu_custom_call" | custom-call | tf_op jit(solution)/shard_map/own_part/pallas_call | solution.py:213
  41.0 0.0 copy-done.1
  41.0 11.0 %sum_part.2 = (bf16[256,2048]{1,0:T(8,128)(2,1)}, bf16[256,2048]{1,0:T(8,128)(2,1)}) custom-call(s32[1]{0:T(128)} %bitcast.3._, f32[2,16,4,8,128]{4,3,2,1,0:T(8,128)} %get-tuple-element.10.vals, s16[2,16,32,128]{3,2,1,0:T(8,128)(2,1)} %get-tuple-element.11.spots, bf16[256,2048]{1,0:T(8,128)(2,1)} %copy-done.1, bf16[256,256]{1,0:T(8,128)(2,1)} %constant.36.clone.li, ...), custom_call_target="tpu_custom_call" | custom-call | tf_op jit(solution)/shard_map/sum_part/pallas_call | solution.py:334
  52.0 4.7 %collective-permute-start = (bf16[256,2048]{1,0:T(8,128)(2,1)}, bf16[256,2048]{1,0:T(8,128)(2,1)}, u32[]{:S(2)}, u32[]{:S(2)}) collective-permute-start(bf16[256,2048]{1,0:T(8,128)(2,1)} %get-tuple-element.12), channel_id=1, source_target_pairs={{0,2},{2,0},{4,6},{6,4},{8,10},{10,8},{12,14},{14,12},{16,18},{18,... | collective-permute-start | bytes 3145736 | tf_op jit(solution)/shard_map/ppermute | solution.py:376
  56.7 0.1 collective-permute-start.3
  56.8 0.0 collective-permute-done.1.weight
  56.8 11.1 %sum_part.3 = (bf16[256,2048]{1,0:T(8,128)(2,1)}, bf16[256,2048]{1,0:T(8,128)(2,1)}) custom-call(s32[1]{0:T(128)} %bitcast.4._, f32[2,16,4,8,128]{4,3,2,1,0:T(8,128)} %get-tuple-element.10.vals, s16[2,16,32,128]{3,2,1,0:T(8,128)(2,1)} %get-tuple-element.11.spots, bf16[256,2048]{1,0:T(8,128)(2,1)} %collective-permute-done.1.weight, ...), custom_call_target="tpu_custom_call" | custom-call | tf_op jit(solution)/shard_map/sum_part/pallas_call | solution.py:334
  67.9 0.0 copy-start.3
  67.9 0.0 copy-start.4
  67.9 0.5 collective-permute-start.2
  68.4 0.0 collective-permute-done
  68.4 1.8 %broadcast_select_fusion.9 = (bf16[256,2048]{1,0:T(8,128)(2,1)S(1)}, bf16[256,2048]{1,0:T(8,128)(2,1)S(1)}) fusion(bf16[256,2048]{1,0:T(8,128)(2,1)} %get-tuple-element.12, bf16[256,2048]{1,0:T(8,128)(2,1)} %collective-permute-done, pred[]{:T(512)S(6)} %eq.6), kind=kLoop, calls=%fused_computation.11 | loop fusion | flops 1048576 | bytes 4194305 | tf_op jit(solution)/shard_map/jit(_where)/select_n | solution.py:377
  70.2 1.5 %pad_maximum_fusion.1 = bf16[256,4096]{1,0:T(8,128)(2,1)} fusion(bf16[256,2048]{1,0:T(8,128)(2,1)S(1)} %get-tuple-element.20, bf16[256,2048]{1,0:T(8,128)(2,1)S(1)} %get-tuple-element.19), kind=kLoop, calls=%fused_computation.1 | loop fusion | flops 4194304 | bytes 4194304 | tf_op jit(solution)/shard_map/concatenate | solution.py:383
  71.8 0.0 collective-permute-done.3
  71.8 0.0 collective-permute-done.2
  71.8 0.0 copy-done.3
  71.8 0.0 copy-done.4
  71.8 1.6 %broadcast_select_fusion.7 = (bf16[256,2048]{1,0:T(8,128)(2,1)S(1)}, bf16[256,2048]{1,0:T(8,128)(2,1)S(1)}, bf16[256,2048]{1,0:T(8,128)(2,1)S(1)}, bf16[256,2048]{1,0:T(8,128)(2,1)S(1)}) fusion(pred[]{:T(512)S(6)} %eq.6, bf16[256,2048]{1,0:T(8,128)(2,1)S(1)} %copy-done.4, bf16[256,2048]{1,0:T(8,128)(2,1)S(1)} %copy-done.3, pred[]{:T(512)S(6)} %eq.7, ...), kind=kLoop, calls=%fused_computation.9 | loop fusion | flops 4194304 | bytes 8388611 | tf_op jit(solution)/shard_map/jit(_where)/select_n | solution.py:377
  73.4 0.0 copy-start.2
  73.4 2.4 %pad_maximum_fusion = bf16[256,8192]{1,0:T(8,128)(2,1)} fusion(bf16[256,2048]{1,0:T(8,128)(2,1)S(1)} %get-tuple-element.18, bf16[256,2048]{1,0:T(8,128)(2,1)S(1)} %get-tuple-element.17, bf16[256,2048]{1,0:T(8,128)(2,1)S(1)} %get-tuple-element.16, bf16[256,2048]{1,0:T(8,128)(2,1)S(1)} %get-tuple-element.15), kind=kLoop, calls=%fused_computation | loop fusion | flops 16777216 | bytes 8388608 | tf_op jit(solution)/shard_map/concatenate | solution.py:394
  75.7 1.3 %copy-done.2 = f32[1,256,4096]{2,1,0:T(8,128)S(1)} copy-done((f32[1,256,4096]{2,1,0:T(8,128)S(1)}, f32[1,256,4096]{2,1,0:T(8,128)}, u32[]{:S(2)}) %copy-start.2) | copy-done | bytes 4194328
  77.1 2.0 %copy.22 = f32[1,256,4096]{2,1,0:T(8,128)} copy(f32[1,256,4096]{2,1,0:T(8,128)S(1)} %copy-done.2) | data formatting | bytes 8388608
Async XLA Ops:
  0.6 1.6 %copy-start = (bf16[256,4096]{1,0:T(8,128)(2,1)S(1)}, bf16[256,4096]{1,0:T(8,128)(2,1)}, u32[]{:S(2)}) copy-start(bf16[256,4096]{1,0:T(8,128)(2,1)} %param.12) | copy-start | bytes 6291460
  2.3 38.7 %copy-start.1 = (bf16[256,2048]{1,0:T(8,128)(2,1)}, bf16[256,2048]{1,0:T(8,128)(2,1)S(1)}, u32[]{:S(2)}) copy-start(bf16[256,2048]{1,0:T(8,128)(2,1)S(1)} %constant_dynamic-slice_fusion.weight) | copy-start | bytes 3145732
  2.3 54.5 %collective-permute-start.1 = (bf16[256,2048]{1,0:T(8,128)(2,1)S(1)}, bf16[256,2048]{1,0:T(8,128)(2,1)}, u32[]{:S(2)}, u32[]{:S(2)}) collective-permute-start(bf16[256,2048]{1,0:T(8,128)(2,1)S(1)} %constant_dynamic-slice_fusion.weight), channel_id=1, source_target_pairs={{0,1},{1,0},{2,3},{3,2},{4,5},{5,4},{6,7},{7,6},{8,9},{9,8},{10,11... | collective-permute-start | bytes 3145736 | tf_op jit(solution)/shard_map/ppermute | solution.py:367
  52.0 16.4 %collective-permute-start = (bf16[256,2048]{1,0:T(8,128)(2,1)}, bf16[256,2048]{1,0:T(8,128)(2,1)}, u32[]{:S(2)}, u32[]{:S(2)}) collective-permute-start(bf16[256,2048]{1,0:T(8,128)(2,1)} %get-tuple-element.12), channel_id=1, source_target_pairs={{0,2},{2,0},{4,6},{6,4},{8,10},{10,8},{12,14},{14,12},{16,18},{18,... | collective-permute-start | bytes 3145736 | tf_op jit(solution)/shard_map/ppermute | solution.py:376
  56.7 15.0 %collective-permute-start.3 = (bf16[256,2048]{1,0:T(8,128)(2,1)}, bf16[256,2048]{1,0:T(8,128)(2,1)}, u32[]{:S(2)}, u32[]{:S(2)}) collective-permute-start(bf16[256,2048]{1,0:T(8,128)(2,1)} %get-tuple-element.14), channel_id=1, source_target_pairs={{0,2},{2,0},{4,6},{6,4},{8,10},{10,8},{12,14},{14,12},{16,18},{18,... | collective-permute-start | bytes 3145736 | tf_op jit(solution)/shard_map/ppermute | solution.py:376
  67.9 3.9 %copy-start.3 = (bf16[256,2048]{1,0:T(8,128)(2,1)S(1)}, bf16[256,2048]{1,0:T(8,128)(2,1)}, u32[]{:S(2)}) copy-start(bf16[256,2048]{1,0:T(8,128)(2,1)} %get-tuple-element.14) | copy-start | bytes 3145732
  67.9 3.9 %copy-start.4 = (bf16[256,2048]{1,0:T(8,128)(2,1)S(1)}, bf16[256,2048]{1,0:T(8,128)(2,1)}, u32[]{:S(2)}) copy-start(bf16[256,2048]{1,0:T(8,128)(2,1)} %get-tuple-element.13) | copy-start | bytes 3145732
  67.9 3.9 %collective-permute-start.2 = (bf16[256,2048]{1,0:T(8,128)(2,1)}, bf16[256,2048]{1,0:T(8,128)(2,1)S(1)}, u32[]{:S(2)}, u32[]{:S(2)}) collective-permute-start(bf16[256,2048]{1,0:T(8,128)(2,1)} %get-tuple-element.13), channel_id=1, source_target_pairs={{0,2},{2,0},{4,6},{6,4},{8,10},{10,8},{12,14},{14,12},{16,18},{18,... | collective-permute-start | bytes 3145736 | tf_op jit(solution)/shard_map/ppermute | solution.py:376
  73.4 3.7 %copy-start.2 = (f32[1,256,4096]{2,1,0:T(8,128)S(1)}, f32[1,256,4096]{2,1,0:T(8,128)}, u32[]{:S(2)}) copy-start(f32[1,256,4096]{2,1,0:T(8,128)} %get-tuple-element.26) | copy-start | bytes 12582916

commit v3 on v2

--- a/solution.py
+++ b/solution.py
@@ -93,11 +93,12 @@
     return a, pos - a * GROUP + lane_offset(topk)
 
 
-def own_kernel(nx, topk, reps, shards, mom, grad, pos, places, lf, rt, li, ri, kept, vals, spots, mine, *sems):
+def own_kernel(nx, topk, reps, shards, mom, grad, pos, lf, rt, li, ri, kept, vals, spots, mine, at_all, places, *sems):
     g, steps = pl.program_id(0), pl.num_programs(0)
     lf, rt, li, ri = lf[...], rt[...], li[...], ri[...]
     tiles = mine.shape[1]
-    chunk = tiles // CHUNKS
+    chunks = min(CHUNKS, tiles)
+    chunk = tiles // chunks
     period = 2 * chunk
     r, s = lax.axis_index("replica"), lax.axis_index("shard")
     me = r * shards + s
@@ -134,15 +135,15 @@
 
     @pl.when(g == 0)
     def _():
-        place_keep().start()
-
-        @pl.loop(1, total)
-        def _(step):
-            place_copy(step).start()
+        for x in range(nx):
+            at_all[pl.ds(x, pos.shape[1], stride=nx)] = pos[x].astype(f32)
+        each = places.shape[1]
+        for half in range(2):
+            places[half] = at_all[half * each : (half + 1) * each].astype(jnp.int32).astype(jnp.int16)
 
     moved = beta_decay * mom[0] + grad[0].astype(f32)
     coeff = right(left(lf, moved), rt)
-    at = pos[0]
+    at = at_all[pl.ds(pl.multiple_of(g * nx, nx), nx)]
     a, b = place(at, topk)
     rows, cols = down(GROUP), down(WIDE)
     picked, own = [], []
@@ -156,13 +157,22 @@
         found = dot(jnp.concatenate([high, low], axis=0), hot_b)
         found = found[:GROUP] + found[GROUP:]
         picked.append(jnp.sum(jnp.where(at_row, found, 0.0), axis=0, keepdims=True))
-    kept[0] = moved - right(left(li, jnp.concatenate(own, axis=0)), ri)
     picked = jnp.concatenate(picked, axis=0)
     half_of, tile_of = g // (2 * tiles), lax.rem(g // 2, tiles)
     mine[half_of, tile_of, pl.ds(pl.multiple_of(lax.rem(g, 2) * nx, nx), nx)] = picked
 
+    kept[0] = moved - right(left(li, jnp.concatenate(own, axis=0)), ri)
+
+    @pl.when(g == 0)
+    def _():
+        place_keep().start()
+
+        @pl.loop(1, total)
+        def _(step):
+            place_copy(step).start()
+
     for half in range(2):
-        for c in range(CHUNKS):
+        for c in range(chunks):
             @pl.when(g == half * 2 * tiles + (c + 1) * period - 1)
             def _(half=half, c=c):
                 @pl.loop(1, total)
@@ -178,7 +188,7 @@
     @pl.when(g == steps - 1)
     def _():
         place_keep().wait()
-        for c in range(CHUNKS):
+        for c in range(chunks):
             value_keep(0, c).wait()
 
         @pl.loop(1, total)
@@ -192,7 +202,7 @@
                 send_sem=place_send.at[step], recv_sem=place_recv.at[step],
                 device_id=(of_r, of_s), device_id_type=MESH,
             ).wait_recv()
-            for c in range(CHUNKS):
+            for c in range(chunks):
                 part = pl.ds(c * chunk, chunk)
                 value_copy(step, 0, c).wait_send()
                 pltpu.make_async_remote_copy(
@@ -202,11 +212,12 @@
                 ).wait_recv()
 
 
-def own_part(mom, grad, pos, places, reps, shards, topk):
+def own_part(mom, grad, pos, reps, shards, topk):
     _, rows, width = mom.shape
     nx = rows // GROUP
     steps = width // WIDE
     tiles = steps // 4
+    chunks = min(CHUNKS, tiles)
     total = reps * shards
     whole = pl.BlockSpec((2 * PAIR, 2 * PAIR), lambda g: (0, 0))
     dma = pltpu.SemaphoreType.DMA
@@ -216,8 +227,7 @@
         in_specs=[
             pl.BlockSpec((1, rows, WIDE), lambda g: (0, 0, g)),
             pl.BlockSpec((1, rows, WIDE), lambda g: (0, 0, g)),
-            pl.BlockSpec((1, nx, LANES), lambda g: (g, 0, 0)),
-            pl.BlockSpec(memory_space=pl.ANY),
+            pl.BlockSpec(pos.shape, lambda g: (0, 0, 0)),
             whole, whole, whole, whole,
         ],
         out_specs=[
@@ -228,17 +238,19 @@
         out_shape=[
             jax.ShapeDtypeStruct((1, rows, width), f32),
             jax.ShapeDtypeStruct((shards, reps, tiles, 2 * nx, LANES), f32),
-            jax.ShapeDtypeStruct((shards, reps) + places.shape[1:], jnp.int16),
+            jax.ShapeDtypeStruct((shards, reps, steps // 2 * nx, LANES), jnp.int16),
         ],
         scratch_shapes=[
             pltpu.VMEM((2, tiles, 2 * nx, LANES), f32),
+            pltpu.VMEM((steps * nx, LANES), f32),
+            pltpu.VMEM((2, steps // 2 * nx, LANES), jnp.int16),
             dma((total,)), dma((total,)), dma,
-            dma((CHUNKS, total)), dma((CHUNKS, total)), dma((CHUNKS,)),
+            dma((chunks, total)), dma((chunks, total)), dma((chunks,)),
         ],
         compiler_params=pltpu.CompilerParams(has_side_effects=True),
         name="own_part",
     )(
-        mom, grad, pos, places,
+        mom, grad, pos,
         left_basis(basis()), right_basis(basis().T),
         left_basis(basis().T), right_basis(basis()),
     )
@@ -293,20 +305,39 @@
     return jnp.concatenate(grid, axis=0)
 
 
-def sum_kernel(nx, topk, reps, _, vals, spots, weight, li, ri, smooth_out, weight_out, sums, at):
+def sum_kernel(nx, topk, reps, first, carries, cuts, held, s, vals, spots, *refs):
+    refs = list(refs)
+    pieces = [refs.pop(0) for _ in cuts]
+    kept_in = refs.pop(0) if carries else None
+    li, ri = refs.pop(0), refs.pop(0)
+    refs = refs[held:]
+    updated_out, weight_out = refs.pop(0), refs.pop(0)
+    smooth_out, direction_out = (refs.pop(0), refs.pop(0)) if first else (None, None)
+    kept_out = refs.pop(0) if carries else None
+    sums, at = refs
     g, last = pl.program_id(0), pl.num_programs(0) - 1
 
     def gather():
         rows = pl.ds(pl.multiple_of(lax.rem(g, 2) * nx, nx), nx)
-        tile = g // 2
+        tile = s[1 + g] // 2
         sums[lax.rem(g, 2)] = scatter(
             nx, topk, [vals[0, r, 0, rows] for r in range(reps)], [at[r, tile, rows] for r in range(reps)]
         )
 
     def finish():
         smooth = jnp.tanh(right(left(li[...], sums[lax.rem(g + 1, 2)]), ri[...]))
-        smooth_out[...] = smooth.astype(bf16)
-        weight_out[...] = (weight[...].astype(f32) - step_rate * smooth).astype(bf16)
+        weight = pieces[0][...]
+        for cut, piece in zip(cuts[1:], pieces[1:]):
+            weight = jnp.where(g > cut, piece[...], weight)
+        updated = (weight.astype(f32) - step_rate * smooth).astype(bf16)
+        updated_out[...] = updated
+        weight_out[...] = updated
+        if first:
+            direction = smooth.astype(bf16)
+            smooth_out[...] = direction
+            direction_out[...] = direction
+        if carries:
+            kept_out[...] = kept_in[...]
 
     @pl.when(g == 0)
     def _():
@@ -324,74 +355,150 @@
         finish()
 
 
-def sum_part(shard, vals, spots, weight, topk):
-    rows, width = weight.shape
+def sum_part(d, scalars, vals, spots, pieces, kept, held, topk):
+    rows, reps, tiles = pieces[0][0].shape[0], vals.shape[1], vals.shape[2]
     nx = rows // GROUP
-    reps, tiles = vals.shape[1:3]
-    steps = width // WIDE
-    column = pl.BlockSpec((rows, WIDE), lambda g, s: (0, jnp.maximum(g - 1, 0)))
+    shards = vals.shape[0]
+    steps = 2 * tiles
+    width = 2 * steps * WIDE
+    first, carries = d == 0, d < 2
+    now = lambda g: jnp.minimum(g, steps - 1)
+    before = lambda g: jnp.maximum(g - 1, 0)
+    cuts, specs = [], []
+    for array, offset, count in pieces:
+        cut = sum(n for _, _, n in pieces[: len(cuts)])
+        cuts.append(cut)
+        if offset:
+            specs.append(pl.BlockSpec((rows, WIDE), lambda g, s: (0, s[1 + steps + before(g)])))
+        else:
+            specs.append(pl.BlockSpec(
+                (rows, WIDE), lambda g, s, cut=cut, n=count: (0, jnp.clip(before(g) - cut, 0, n - 1))
+            ))
     whole = pl.BlockSpec((2 * PAIR, 2 * PAIR), lambda g, s: (0, 0))
+    column = lambda at: pl.BlockSpec((rows, WIDE), lambda g, s: (0, s[1 + at * steps + before(g)]))
+    kept_spec = pl.BlockSpec((1, rows, WIDE), lambda g, s: (0, 0, d * steps + before(g)))
+    in_specs = [
+        pl.BlockSpec((1, reps, 1, 2 * nx, LANES), lambda g, s: (s[0], 0, s[1 + now(g)] // 2, 0, 0)),
+        pl.BlockSpec((1,) + spots.shape[1:], lambda g, s: (s[0], 0, 0, 0)),
+    ] + specs + ([kept_spec] if carries else []) + [whole, whole]
+    in_specs += [pl.BlockSpec(memory_space=pl.ANY)] * len(held)
+    half = jax.ShapeDtypeStruct((rows, width // 2), bf16)
+    out_specs, out_shape = [column(0), column(2)], [half, jax.ShapeDtypeStruct((rows, shards * width), bf16)]
+    if first:
+        out_specs += [column(0), column(1)]
+        out_shape += [half, jax.ShapeDtypeStruct((rows, width), bf16)]
+    if carries:
+        out_specs.append(kept_spec)
+        out_shape.append(jax.ShapeDtypeStruct((1, rows, width), f32))
+    at = 1 + len(in_specs) - len(held)
+    targets = [1, 2][: len(held)]
     return pl.pallas_call(
-        functools.partial(sum_kernel, nx, topk, reps),
+        functools.partial(sum_kernel, nx, topk, reps, first, carries, cuts, len(held)),
         grid_spec=pltpu.PrefetchScalarGridSpec(
             num_scalar_prefetch=1,
             grid=(steps + 1,),
-            in_specs=[
-                pl.BlockSpec(
-                    (1, reps, 1, 2 * nx, LANES),
-                    lambda g, s: (s[0], 0, jnp.minimum(g, steps - 1) // 2, 0, 0),
-                ),
-                pl.BlockSpec((1,) + spots.shape[1:], lambda g, s: (s[0], 0, 0, 0)),
-                column, whole, whole,
-            ],
-            out_specs=[column, column],
+            in_specs=in_specs,
+            out_specs=out_specs,
             scratch_shapes=[
                 pltpu.VMEM((2, rows, WIDE), f32), pltpu.VMEM((reps, tiles, 2 * nx, LANES), f32),
             ],
         ),
-        out_shape=[jax.ShapeDtypeStruct((rows, width), bf16)] * 2,
+        out_shape=out_shape,
+        input_output_aliases={at + i: t for i, t in enumerate(targets)},
+        cost_estimate=pl.CostEstimate(flops=steps * 2 * 10**9, bytes_accessed=8 * 2**20, transcendentals=0),
         name="sum_part",
-    )(shard, vals, spots, weight, left_basis(basis().T), right_basis(basis()))
+    )(
+        scalars, vals, spots, *[array for array, _, _ in pieces], *([kept] if carries else []),
+        left_basis(basis().T), right_basis(basis()), *held,
+    )
+
+
+def place_kernel(count, _, *refs):
+    for i in range(count):
+        refs[2 * count + i][...] = refs[i][...]
+
+
+def put(blocks, parts, fulls):
+    rows, width = parts[0].shape
+    wide = math.gcd(width, 1024)
+    count, steps = len(parts), width // wide
+    def spec(i):
+        return pl.BlockSpec((rows, wide), lambda g, s: (0, s[i] * steps + g))
+    return pl.pallas_call(
+        functools.partial(place_kernel, count),
+        grid_spec=pltpu.PrefetchScalarGridSpec(
+            num_scalar_prefetch=1,
+            grid=(steps,),
+            in_specs=[pl.BlockSpec((rows, wide), lambda g, s: (0, g))] * count
+            + [pl.BlockSpec(memory_space=pl.ANY)] * count,
+            out_specs=[spec(i) for i in range(count)],
+        ),
+        out_shape=[jax.ShapeDtypeStruct(f.shape, f.dtype) for f in fulls],
+        input_output_aliases={1 + count + i: i for i in range(count)},
+        cost_estimate=pl.CostEstimate(flops=0, bytes_accessed=4 * count * rows * width, transcendentals=0),
+        name="put",
+    )(blocks, *parts, *fulls)
 
 
 def per_device(reps, shards, weight, momentum, grad, positions):
     rows, width = weight.shape
     _, nx, ny, topk = positions.shape
     half = width // 2
-    steps = width // WIDE
+    steps = half // WIDE
     r, s = lax.axis_index("replica"), lax.axis_index("shard")
     core = lax.rem(r, 2)
-
-    mine_w = lax.dynamic_slice(weight, (0, core * half), (rows, half))
-    weights = [mine_w] + [
-        lax.ppermute(mine_w, "shard", [(i, (i + d) % shards) for i in range(shards)])
-        for d in range(1, shards)
-    ]
-
-    pos = positions[0].reshape(nx, steps, LANES).transpose(1, 0, 2)
-    places = pos.astype(jnp.int16).reshape(2, steps // 2 * nx, LANES)
-    kept, vals, spots = own_part(momentum, grad, pos.astype(f32), places, reps, shards, topk)
-
-    pairs = [(i, i ^ 1) for i in range(reps)]
-    flip = lambda x: lax.ppermute(x, "replica", pairs)
-    order = lambda a, b: [jnp.where(core == 0, a, b), jnp.where(core == 0, b, a)]
-    pieces, direction = [], None
-    for d in range(shards):
+    spread = reps % 8 == 0 and steps % 4 == 0
+    side = ((r // 2) + (r // 4)) % 2 if spread else 0 * r
+
+    def ring(x, d):
+        return lax.ppermute(x, "shard", [(i, (i + d) % shards) for i in range(shards)])
+
+    def across(x, bit):
+        return lax.ppermute(x, "replica", [(i, i ^ bit) for i in range(reps)])
+
+    others = []
+    units = np.arange(steps)
+    if spread:
+        part = half // 2
+        mine = lax.dynamic_slice(weight, (0, core * half + side * part), (rows, part))
+        for d in range(1, shards):
+            near = ring(mine, d)
+            others.append((near, across(near[:, : part // 2], 2), across(near[:, part // 2 :], 4)))
+        order = (units + side * (steps // 2)) % steps
+    else:
+        mine = lax.dynamic_slice(weight, (0, core * half), (rows, half))
+        others = [(ring(mine, d),) for d in range(1, shards)]
+        order = jnp.asarray(units)
+
+    pos = positions[0].reshape(nx, 2 * steps, LANES)
+    kept, vals, spots = own_part(momentum, grad, pos, reps, shards, topk)
+
+    def scalars(of, order):
+        base = core * steps + order
+        return jnp.concatenate([of.reshape(1), order, base, of * 2 * steps + base]).astype(jnp.int32)
+
+    updated, new_weight, smooth, direction, kept_full = sum_part(
+        0, scalars(s, jnp.asarray(units)), vals, spots, [(weight, True, steps)], kept, (), topk
+    )
+    parts = [(s, updated)]
+    for d in range(1, shards):
         of = lax.rem(s - d + shards, shards)
-        smooth, updated = sum_part(of.reshape(1).astype(jnp.int32), vals, spots, weights[d], topk)
-        if d == 0:
-            direction = jnp.concatenate(order(smooth, flip(smooth)), axis=1)
-        pieces.append((updated, flip(updated)))
-
-    columns = []
-    for t in range(shards):
-        d = lax.rem(s - t + shards, shards)
-        a, b = pieces[0]
-        for e in range(1, shards):
-            a = jnp.where(d == e, pieces[e][0], a)
-            b = jnp.where(d == e, pieces[e][1], b)
-        columns += order(a, b)
-    return (kept, direction, jnp.concatenate(columns, axis=1))
+        pieces = [(w, False, w.shape[1] // WIDE) for w in others[d - 1]]
+        held = (new_weight, kept_full) if d == 1 else (new_weight,)
+        out = sum_part(d, scalars(of, order), vals, spots, pieces, kept, held, topk)
+        updated, new_weight = out[0], out[1]
+        if d == 1:
+            kept_full = out[2]
+        parts.append((of, updated))
+
+    far = 1 - core
+    block = lambda *at: jnp.stack(at).astype(jnp.int32)
+    new_weight, direction = put(
+        block(s * 2 + far, far), [across(parts[0][1], 1), across(smooth, 1)], [new_weight, direction]
+    )
+    for of, piece in parts[1:]:
+        new_weight, = put(block(of * 2 + far), [across(piece, 1)], [new_weight])
+    return (kept_full, direction, new_weight)
 
 
 def solution(mesh):

time: 79.6 us -> 88.9 us (1.12)
  Pallas kernels: 55.2 us -> 63.6 us
  waiting for transfers between devices: 0.01 us -> 7.09 us
  other arithmetic: 8.17 us -> 1.92 us
  local copies, waits for them, and re-layouts: 6.67 us -> 5.12 us
  starting transfers between devices: 8.32 us -> 9.85 us
    pallas_call x2 -> x4, Pallas kernels: 22.1 us -> 30.9 us  [the longest x2 25.6 us: sum_part(): pl.pallas_call(functools.partial(sum_kernel, nx, topk, reps, first, carri...]
    ppermute x4 -> x6, waiting for transfers between devices: 0.01 us -> 7.09 us  [the longest x5 7.09 us: across(): return lax.ppermute(x, 'replica', [(i, i ^ bit) for i in range(reps)])]
    select_n x2 -> x1, other arithmetic: 3.35 us -> 0.01 us  [per_device(): order = (units + side * (steps // 2)) % steps]
    concatenate x2, other arithmetic: 3.89 us -> 1.3 us  [scalars(): jnp.concatenate([of.reshape(1), order, base, of * 2 * steps + base])]
    unnamed x11, local copies, waits for them, and re-layouts: 4.95 us -> 3.29 us
    convert_element_type x6 -> x0, local copies, waits for them, and re-layouts: 1.65 us -> none  [the longest x3 0.84 us: per_device(): places = pos.astype(jnp.int16).reshape(2, steps // 2 * nx, LANES)]
    ppermute x4 -> x6, starting transfers between devices: 8.32 us -> 9.85 us  [the longest x5 6.82 us: across(): return lax.ppermute(x, 'replica', [(i, i ^ bit) for i in range(reps)])]
    dynamic_slice x1, local copies, waits for them, and re-layouts: 0.07 us -> 1.08 us  [per_device(): lax.dynamic_slice(weight, (0, core * half + side * part), (rows, part))]
  transfers between devices with their start and end apart: 4 -> 6, of which waited for: 0 -> 2; matrix products, arithmetic and copies ran while one was open for 7% -> 4% of each run, Pallas kernels for 70% -> 70%
where the time goes in v3:
time: 88.9 us; the launch traced here: 88.3 us
  Pallas kernels  63.6 us (72%)
  starting transfers between devices  9.85 us (11%)
  waiting for transfers between devices  7.09 us (8%)
  local copies, waits for them, and re-layouts  5.12 us (6%)
  other arithmetic  1.92 us (2%)
    pallas_call x1, Pallas kernels, own_part(): pl.pallas_call(functools.partial(own_kernel, nx, topk, reps, shards), gri...  32.7 us
    pallas_call x2, Pallas kernels, sum_part(): pl.pallas_call(functools.partial(sum_kernel, nx, topk, reps, first, carri...  25.6 us
    ppermute x5, waiting for transfers between devices, across(): return lax.ppermute(x, 'replica', [(i, i ^ bit) for i in range(reps)])  7.09 us
    ppermute x5, starting transfers between devices, across(): return lax.ppermute(x, 'replica', [(i, i ^ bit) for i in range(reps)])  6.82 us
    pallas_call x2, Pallas kernels, put(): pl.pallas_call(functools.partial(place_kernel, count), grid_spec=pltpu.Pr...  5.31 us
    unnamed x11, local copies, waits for them, and re-layouts  3.29 us
    ppermute x1, starting transfers between devices, ring(): lax.ppermute(x, 'shard', [(i, (i + d) % shards) for i in range(shards)])  3.03 us
  transfers between devices with their start and end apart: 6, of which 2 were waited for; matrix products, arithmetic and copies ran while one was open for 4% of the time, Pallas kernels for 70%

profile of v3, /device:TPU:0, one launch (start us, length us, event | category | flops | bytes accessed | tf_op | source)
XLA Modules:
  0.0 88.3 jit_solution(11383017667705870413)
XLA Ops:
  0.7 1.1 %constant_dynamic-slice_fusion = bf16[256,1024]{1,0:T(8,128)(2,1)S(1)} fusion(bf16[256,4096]{1,0:T(8,128)(2,1)} %refs_0_.1, s32[]{:T(128)S(6)} %select_n.27), kind=kLoop, calls=%fused_computation.11 | loop fusion | bytes 1048580 | tf_op jit(solution)/shard_map/dynamic_slice | solution.py:463
  1.8 3.0 %collective-permute-start = (bf16[256,1024]{1,0:T(8,128)(2,1)S(1)}, bf16[256,1024]{1,0:T(8,128)(2,1)S(1)}, u32[]{:S(2)}, u32[]{:S(2)}) collective-permute-start(bf16[256,1024]{1,0:T(8,128)(2,1)S(1)} %constant_dynamic-slice_fusion), channel_id=1, source_target_pairs={{0,1},{1,0},{2,3},{3,2},{4,5},{5,4},{6,7},{7,6},{8,9},{9,8},{10,11... | collective-permute-start | bytes 1572872 | tf_op jit(solution)/shard_map/ppermute | solution.py:454
  4.8 0.9 %copy.22 = s32[1,4,64,32]{3,2,1,0:T(8,128)S(1)} copy(s32[1,4,64,32]{2,3,1,0:T(8,128)} %param.16) | data formatting | bytes 65536 | tf_op args[3]
  5.7 0.7 reshape_squeeze.3.pos
  6.4 0.7 pad_add_fusion.1.s
  7.1 32.7 %own_part.1 = (f32[1,256,4096]{2,1,0:T(8,128)}, f32[2,16,4,8,128]{4,3,2,1,0:T(8,128)}, s16[2,16,32,128]{3,2,1,0:T(8,128)(2,1)}) custom-call(f32[1,256,4096]{2,1,0:T(8,128)} %mom.1, bf16[1,256,4096]{2,1,0:T(8,128)(2,1)} %grad.1, s32[4,16,128]{2,1,0:T(8,128)} %reshape_squeeze.3.pos, bf16[256,256]{1,0:T(8,128)(2,1)} %constant.82.clone.lf, ...), custom_call_target="tpu_custom_call" | custom-call | tf_op jit(solution)/shard_map/own_part/pallas_call | solution.py:224
  39.8 12.8 %sum_part.2 = (bf16[256,2048]{1,0:T(8,128)(2,1)}, bf16[256,8192]{1,0:T(8,128)(2,1)}, bf16[256,2048]{1,0:T(8,128)(2,1)}, bf16[256,4096]{1,0:T(8,128)(2,1)}, f32[1,256,4096]{2,1,0:T(8,128)}) custom-call(s32[25]{0:T(128)} %pad_add_fusion.1.s, f32[2,16,4,8,128]{4,3,2,1,0:T(8,128)} %get-tuple-element.16.vals, s16[2,16,32,128]{3,2,1,0:T(8,128)(2,1)} %get-tuple-element.17.spots, ...), custom_call_target="tpu_custom_call" | custom-call | flops 16000000000 | bytes 8388608 | tf_op jit(solution)/shard_map/sum_part/pallas_call | solution.py:395
  52.6 4.7 %collective-permute-start.3 = (bf16[256,2048]{1,0:T(8,128)(2,1)}, bf16[256,2048]{1,0:T(8,128)(2,1)S(1)}, u32[]{:S(2)}, u32[]{:S(2)}) collective-permute-start(bf16[256,2048]{1,0:T(8,128)(2,1)} %get-tuple-element.22), channel_id=1, source_target_pairs={{0,2},{2,0},{4,6},{6,4},{8,10},{10,8},{12,14},{14,12},{16,18},{18,... | collective-permute-start | bytes 3145736 | tf_op jit(solution)/shard_map/ppermute | solution.py:457
  57.3 0.1 collective-permute-start.4
  57.4 0.0 collective-permute-done.refs_0_
  57.4 0.0 copy-start.3
  57.4 1.3 %collective-permute-start.2 = (bf16[256,512]{1,0:T(8,128)(2,1)S(1)}, bf16[256,512]{1,0:T(8,128)(2,1)S(1)}, u32[]{:S(2)}, u32[]{:S(2)}) collective-permute-start(bf16[256,512]{1,0:T(8,128)(2,1)S(1)} %get-tuple-element.31), channel_id=1, source_target_pairs={{0,8},{2,10},{4,12},{6,14},{8,0},{10,2},{12,4},{14,6},{16,24},{18,... | collective-permute-start | bytes 786440 | tf_op jit(solution)/shard_map/ppermute | solution.py:457
  58.7 0.7 collective-permute-start.1
  59.5 0.6 pad_add_fusion.s
  60.1 6.0 %collective-permute-done.2.refs_2_ = bf16[256,512]{1,0:T(8,128)(2,1)S(1)} collective-permute-done((bf16[256,512]{1,0:T(8,128)(2,1)S(1)}, bf16[256,512]{1,0:T(8,128)(2,1)S(1)}, u32[]{:S(2)}, u32[]{:S(2)}) %collective-permute-start.2) | collective-permute-done | bytes 262176 | tf_op jit(solution)/shard_map/ppermute | solution.py:457
  66.2 0.0 copy-start.4
  66.2 1.0 %collective-permute-done.1.refs_1_ = bf16[256,512]{1,0:T(8,128)(2,1)} collective-permute-done((bf16[256,512]{1,0:T(8,128)(2,1)S(1)}, bf16[256,512]{1,0:T(8,128)(2,1)}, u32[]{:S(2)}, u32[]{:S(2)}) %collective-permute-start.1) | collective-permute-done | bytes 262176 | tf_op jit(solution)/shard_map/ppermute | solution.py:457
  67.2 0.0 copy-done.3
  67.2 0.0 copy-done.4
  67.2 12.8 %sum_part.3 = (bf16[256,2048]{1,0:T(8,128)(2,1)}, bf16[256,8192]{1,0:T(8,128)(2,1)}, f32[1,256,4096]{2,1,0:T(8,128)}) custom-call(s32[25]{0:T(128)} %pad_add_fusion.s, f32[2,16,4,8,128]{4,3,2,1,0:T(8,128)} %get-tuple-element.16.vals, s16[2,16,32,128]{3,2,1,0:T(8,128)(2,1)} %get-tuple-element.17.spots, ...), custom_call_target="tpu_custom_call", output_to_operand_aliasing={{1}: (9, {}), {2}: (10, {})} | custom-call | flops 16000000000 | bytes 8388608 | tf_op jit(solution)/shard_map/sum_part/pallas_call | solution.py:395
  80.0 0.0 collective-permute-start.5
  80.1 0.6 pad_add_fusion.2._
  80.6 0.0 collective-permute-done.3.refs_0_
  80.6 0.0 copy-start
  80.7 0.0 collective-permute-done.4.refs_1_
  80.7 0.0 copy-start.1
  80.7 1.0 %copy-done = bf16[256,2048]{1,0:T(8,128)(2,1)} copy-done((bf16[256,2048]{1,0:T(8,128)(2,1)}, bf16[256,2048]{1,0:T(8,128)(2,1)S(1)}, u32[]{:S(2)}) %copy-start) | copy-done | bytes 1048600
  81.7 0.4 copy-done.1
  82.0 3.3 %put.2 = (bf16[256,8192]{1,0:T(8,128)(2,1)}, bf16[256,4096]{1,0:T(8,128)(2,1)}) custom-call(s32[2]{0:T(128)} %pad_add_fusion.2._, bf16[256,2048]{1,0:T(8,128)(2,1)} %copy-done, bf16[256,2048]{1,0:T(8,128)(2,1)} %copy-done.1, bf16[256,8192]{1,0:T(8,128)(2,1)} %get-tuple-element.24.refs_2_, ...), custom_call_target="tpu_custom_call", output_to_operand_aliasing={{0}: (3, {}), {1}: (4, {})} | custom-call | bytes 4194304 | tf_op jit(solution)/shard_map/put/pallas_call | solution.py:427
  85.3 0.0 collective-permute-done.5.refs_0_
  85.3 0.0 copy-start.2
  85.3 1.0 %copy-done.2 = bf16[256,2048]{1,0:T(8,128)(2,1)} copy-done((bf16[256,2048]{1,0:T(8,128)(2,1)}, bf16[256,2048]{1,0:T(8,128)(2,1)S(1)}, u32[]{:S(2)}) %copy-start.2) | copy-done | bytes 1048600
  86.3 2.0 %put.3 = bf16[256,8192]{1,0:T(8,128)(2,1)} custom-call(s32[1]{0:T(128)} %bitcast.4._, bf16[256,2048]{1,0:T(8,128)(2,1)} %copy-done.2, bf16[256,8192]{1,0:T(8,128)(2,1)} %get-tuple-element.28.refs_1_), custom_call_target="tpu_custom_call", output_to_operand_aliasing={{}: (2, {})} | custom-call | bytes 2097152 | tf_op jit(solution)/shard_map/put/pallas_call | solution.py:427
  (5 shorter events, 0.1 us)
Async XLA Ops:
  1.8 55.6 %collective-permute-start = (bf16[256,1024]{1,0:T(8,128)(2,1)S(1)}, bf16[256,1024]{1,0:T(8,128)(2,1)S(1)}, u32[]{:S(2)}, u32[]{:S(2)}) collective-permute-start(bf16[256,1024]{1,0:T(8,128)(2,1)S(1)} %constant_dynamic-slice_fusion), channel_id=1, source_target_pairs={{0,1},{1,0},{2,3},{3,2},{4,5},{5,4},{6,7},{7,6},{8,9},{9,8},{10,11... | collective-permute-start | bytes 1572872 | tf_op jit(solution)/shard_map/ppermute | solution.py:454
  52.6 28.0 %collective-permute-start.3 = (bf16[256,2048]{1,0:T(8,128)(2,1)}, bf16[256,2048]{1,0:T(8,128)(2,1)S(1)}, u32[]{:S(2)}, u32[]{:S(2)}) collective-permute-start(bf16[256,2048]{1,0:T(8,128)(2,1)} %get-tuple-element.22), channel_id=1, source_target_pairs={{0,2},{2,0},{4,6},{6,4},{8,10},{10,8},{12,14},{14,12},{16,18},{18,... | collective-permute-start | bytes 3145736 | tf_op jit(solution)/shard_map/ppermute | solution.py:457
  57.3 23.3 %collective-permute-start.4 = (bf16[256,2048]{1,0:T(8,128)(2,1)}, bf16[256,2048]{1,0:T(8,128)(2,1)S(1)}, u32[]{:S(2)}, u32[]{:S(2)}) collective-permute-start(bf16[256,2048]{1,0:T(8,128)(2,1)} %get-tuple-element.23), channel_id=1, source_target_pairs={{0,2},{2,0},{4,6},{6,4},{8,10},{10,8},{12,14},{14,12},{16,18},{18,... | collective-permute-start | bytes 3145736 | tf_op jit(solution)/shard_map/ppermute | solution.py:457
  57.4 9.8 %copy-start.3 = (bf16[256,1024]{1,0:T(8,128)(2,1)}, bf16[256,1024]{1,0:T(8,128)(2,1)S(1)}, u32[]{:S(2)}) copy-start(bf16[256,1024]{1,0:T(8,128)(2,1)S(1)} %collective-permute-done.refs_0_) | copy-start | bytes 1572868
  57.4 8.7 %collective-permute-start.2 = (bf16[256,512]{1,0:T(8,128)(2,1)S(1)}, bf16[256,512]{1,0:T(8,128)(2,1)S(1)}, u32[]{:S(2)}, u32[]{:S(2)}) collective-permute-start(bf16[256,512]{1,0:T(8,128)(2,1)S(1)} %get-tuple-element.31), channel_id=1, source_target_pairs={{0,8},{2,10},{4,12},{6,14},{8,0},{10,2},{12,4},{14,6},{16,24},{18,... | collective-permute-start | bytes 786440 | tf_op jit(solution)/shard_map/ppermute | solution.py:457
  58.7 8.5 %collective-permute-start.1 = (bf16[256,512]{1,0:T(8,128)(2,1)S(1)}, bf16[256,512]{1,0:T(8,128)(2,1)}, u32[]{:S(2)}, u32[]{:S(2)}) collective-permute-start(bf16[256,512]{1,0:T(8,128)(2,1)S(1)} %get-tuple-element.32), channel_id=1, source_target_pairs={{0,4},{2,6},{4,0},{6,2},{8,12},{10,14},{12,8},{14,10},{16,20},{18,... | collective-permute-start | bytes 786440 | tf_op jit(solution)/shard_map/ppermute | solution.py:457
  66.2 1.0 %copy-start.4 = (bf16[256,512]{1,0:T(8,128)(2,1)}, bf16[256,512]{1,0:T(8,128)(2,1)S(1)}, u32[]{:S(2)}) copy-start(bf16[256,512]{1,0:T(8,128)(2,1)S(1)} %collective-permute-done.2.refs_2_) | copy-start | bytes 786436
  80.0 5.3 %collective-permute-start.5 = (bf16[256,2048]{1,0:T(8,128)(2,1)}, bf16[256,2048]{1,0:T(8,128)(2,1)S(1)}, u32[]{:S(2)}, u32[]{:S(2)}) collective-permute-start(bf16[256,2048]{1,0:T(8,128)(2,1)} %get-tuple-element.27), channel_id=1, source_target_pairs={{0,2},{2,0},{4,6},{6,4},{8,10},{10,8},{12,14},{14,12},{16,18},{18,... | collective-permute-start | bytes 3145736 | tf_op jit(solution)/shard_map/ppermute | solution.py:457
  80.6 1.0 %copy-start = (bf16[256,2048]{1,0:T(8,128)(2,1)}, bf16[256,2048]{1,0:T(8,128)(2,1)S(1)}, u32[]{:S(2)}) copy-start(bf16[256,2048]{1,0:T(8,128)(2,1)S(1)} %collective-permute-done.3.refs_0_) | copy-start | bytes 3145732
  80.7 1.4 %copy-start.1 = (bf16[256,2048]{1,0:T(8,128)(2,1)}, bf16[256,2048]{1,0:T(8,128)(2,1)S(1)}, u32[]{:S(2)}) copy-start(bf16[256,2048]{1,0:T(8,128)(2,1)S(1)} %collective-permute-done.4.refs_1_) | copy-start | bytes 3145732
  85.3 1.0 %copy-start.2 = (bf16[256,2048]{1,0:T(8,128)(2,1)}, bf16[256,2048]{1,0:T(8,128)(2,1)S(1)}, u32[]{:S(2)}) copy-start(bf16[256,2048]{1,0:T(8,128)(2,1)S(1)} %collective-permute-done.5.refs_0_) | copy-start | bytes 3145732

commit v4 on v3

--- a/solution.py
+++ b/solution.py
@@ -13,7 +13,6 @@
 LANES = 128
 WIDE = 256
 PAIR = 128
-CHUNKS = 2
 
 beta_decay = 0.9
 step_rate = 0.02
@@ -93,13 +92,16 @@
     return a, pos - a * GROUP + lane_offset(topk)
 
 
+def cut_points(tiles):
+    return sorted({0, tiles // 2, tiles - 1, tiles} - {-1})
+
+
 def own_kernel(nx, topk, reps, shards, mom, grad, pos, lf, rt, li, ri, kept, vals, spots, mine, at_all, places, *sems):
     g, steps = pl.program_id(0), pl.num_programs(0)
     lf, rt, li, ri = lf[...], rt[...], li[...], ri[...]
     tiles = mine.shape[1]
-    chunks = min(CHUNKS, tiles)
-    chunk = tiles // chunks
-    period = 2 * chunk
+    cuts = cut_points(tiles)
+    chunks = len(cuts) - 1
     r, s = lax.axis_index("replica"), lax.axis_index("shard")
     me = r * shards + s
     total = reps * shards
@@ -119,7 +121,7 @@
 
     def value_copy(step, half, c):
         to_r, to_s = peer(step)
-        part = pl.ds(c * chunk, chunk)
+        part = pl.ds(cuts[c], cuts[c + 1] - cuts[c])
         return pltpu.make_async_remote_copy(
             src_ref=mine.at[half, part], dst_ref=vals.at[s, r, part],
             send_sem=send_sem.at[c, step], recv_sem=recv_sem.at[c, step],
@@ -130,11 +132,17 @@
         return pltpu.make_async_copy(places.at[lax.rem(r, 2)], spots.at[s, r], place_own)
 
     def value_keep(half, c):
-        part = pl.ds(c * chunk, chunk)
+        part = pl.ds(cuts[c], cuts[c + 1] - cuts[c])
         return pltpu.make_async_copy(mine.at[half, part], vals.at[s, r, part], own_sem.at[c])
 
     @pl.when(g == 0)
     def _():
+        barrier = pltpu.get_barrier_semaphore()
+
+        @pl.loop(1, total)
+        def _(step):
+            pl.semaphore_signal(barrier, inc=1, device_id=peer(step), device_id_type=MESH)
+
         for x in range(nx):
             at_all[pl.ds(x, pos.shape[1], stride=nx)] = pos[x].astype(f32)
         each = places.shape[1]
@@ -165,6 +173,7 @@
 
     @pl.when(g == 0)
     def _():
+        pl.semaphore_wait(pltpu.get_barrier_semaphore(), total - 1)
         place_keep().start()
 
         @pl.loop(1, total)
@@ -173,7 +182,7 @@
 
     for half in range(2):
         for c in range(chunks):
-            @pl.when(g == half * 2 * tiles + (c + 1) * period - 1)
+            @pl.when(g == 2 * (half * tiles + cuts[c + 1]) - 1)
             def _(half=half, c=c):
                 @pl.loop(1, total)
                 def _(step):
@@ -203,7 +212,7 @@
                 device_id=(of_r, of_s), device_id_type=MESH,
             ).wait_recv()
             for c in range(chunks):
-                part = pl.ds(c * chunk, chunk)
+                part = pl.ds(cuts[c], cuts[c + 1] - cuts[c])
                 value_copy(step, 0, c).wait_send()
                 pltpu.make_async_remote_copy(
                     src_ref=mine.at[0, part], dst_ref=vals.at[of_s, of_r, part],
@@ -217,7 +226,7 @@
     nx = rows // GROUP
     steps = width // WIDE
     tiles = steps // 4
-    chunks = min(CHUNKS, tiles)
+    chunks = len(cut_points(tiles)) - 1
     total = reps * shards
     whole = pl.BlockSpec((2 * PAIR, 2 * PAIR), lambda g: (0, 0))
     dma = pltpu.SemaphoreType.DMA
@@ -247,7 +256,7 @@
             dma((total,)), dma((total,)), dma,
             dma((chunks, total)), dma((chunks, total)), dma((chunks,)),
         ],
-        compiler_params=pltpu.CompilerParams(has_side_effects=True),
+        compiler_params=pltpu.CompilerParams(has_side_effects=True, collective_id=0),
         name="own_part",
     )(
         mom, grad, pos,
@@ -305,7 +314,7 @@
     return jnp.concatenate(grid, axis=0)
 
 
-def sum_kernel(nx, topk, reps, first, carries, cuts, held, s, vals, spots, *refs):
+def sum_kernel(nx, topk, reps, first, carries, base, cuts, held, s, vals, spots, *refs):
     refs = list(refs)
     pieces = [refs.pop(0) for _ in cuts]
     kept_in = refs.pop(0) if carries else None
@@ -314,7 +323,7 @@
     updated_out, weight_out = refs.pop(0), refs.pop(0)
     smooth_out, direction_out = (refs.pop(0), refs.pop(0)) if first else (None, None)
     kept_out = refs.pop(0) if carries else None
-    sums, at = refs
+    sums, at, hold, in_sem, out_sem = refs
     g, last = pl.program_id(0), pl.num_programs(0) - 1
 
     def gather():
@@ -336,8 +345,31 @@
             direction = smooth.astype(bf16)
             smooth_out[...] = direction
             direction_out[...] = direction
-        if carries:
-            kept_out[...] = kept_in[...]
+
+    def column(step):
+        return pl.ds(pl.multiple_of((base + step) * WIDE, WIDE), WIDE)
+
+    def bring(step):
+        slot = lax.rem(step, 2)
+        return pltpu.make_async_copy(kept_in.at[0, :, column(step)], hold.at[slot], in_sem.at[slot])
+
+    def drop(step):
+        slot = lax.rem(step, 2)
+        return pltpu.make_async_copy(hold.at[slot], kept_out.at[0, :, column(step)], out_sem.at[slot])
+
+    if carries:
+        @pl.when((g > 1) & (g < last))
+        def _():
+            drop(g - 2).wait()
+
+        @pl.when(g < last)
+        def _():
+            bring(g).start()
+
+        @pl.when(g > 0)
+        def _():
+            bring(g - 1).wait()
+            drop(g - 1).start()
 
     @pl.when(g == 0)
     def _():
@@ -353,6 +385,9 @@
     @pl.when(g == last)
     def _():
         finish()
+        if carries:
+            drop(g - 2).wait()
+            drop(g - 1).wait()
 
 
 def sum_part(d, scalars, vals, spots, pieces, kept, held, topk):
@@ -376,7 +411,7 @@
             ))
     whole = pl.BlockSpec((2 * PAIR, 2 * PAIR), lambda g, s: (0, 0))
     column = lambda at: pl.BlockSpec((rows, WIDE), lambda g, s: (0, s[1 + at * steps + before(g)]))
-    kept_spec = pl.BlockSpec((1, rows, WIDE), lambda g, s: (0, 0, d * steps + before(g)))
+    kept_spec = pl.BlockSpec(memory_space=pl.ANY)
     in_specs = [
         pl.BlockSpec((1, reps, 1, 2 * nx, LANES), lambda g, s: (s[0], 0, s[1 + now(g)] // 2, 0, 0)),
         pl.BlockSpec((1,) + spots.shape[1:], lambda g, s: (s[0], 0, 0, 0)),
@@ -393,7 +428,7 @@
     at = 1 + len(in_specs) - len(held)
     targets = [1, 2][: len(held)]
     return pl.pallas_call(
-        functools.partial(sum_kernel, nx, topk, reps, first, carries, cuts, len(held)),
+        functools.partial(sum_kernel, nx, topk, reps, first, carries, d * steps, cuts, len(held)),
         grid_spec=pltpu.PrefetchScalarGridSpec(
             num_scalar_prefetch=1,
             grid=(steps + 1,),
@@ -401,6 +436,7 @@
             out_specs=out_specs,
             scratch_shapes=[
                 pltpu.VMEM((2, rows, WIDE), f32), pltpu.VMEM((reps, tiles, 2 * nx, LANES), f32),
+                pltpu.VMEM((2, rows, WIDE), f32), pltpu.SemaphoreType.DMA((2,)), pltpu.SemaphoreType.DMA((2,)),
             ],
         ),
         out_shape=out_shape,
@@ -413,31 +449,36 @@
     )
 
 
-def place_kernel(count, _, *refs):
+def place_kernel(count, shards, blocks, *refs):
+    r, s = lax.axis_index("replica"), lax.axis_index("shard")
+    far = 1 - lax.rem(r, 2)
+    sems = refs[-1]
+    copies = []
     for i in range(count):
-        refs[2 * count + i][...] = refs[i][...]
-
-
-def put(blocks, parts, fulls):
-    rows, width = parts[0].shape
-    wide = math.gcd(width, 1024)
-    count, steps = len(parts), width // wide
-    def spec(i):
-        return pl.BlockSpec((rows, wide), lambda g, s: (0, s[i] * steps + g))
+        part, full = refs[i], refs[2 * count + i]
+        width = part.shape[1]
+        block = far if blocks[i] is None else 2 * lax.rem(s + blocks[i], shards) + far
+        at = pl.ds(pl.multiple_of(block * width, width), width)
+        copies.append(pltpu.make_async_copy(part, full.at[:, at], sems.at[i]))
+    for copy in copies:
+        copy.start()
+    for copy in copies:
+        copy.wait()
+
+
+def put(shards, blocks, parts, fulls):
+    count = len(parts)
     return pl.pallas_call(
-        functools.partial(place_kernel, count),
-        grid_spec=pltpu.PrefetchScalarGridSpec(
-            num_scalar_prefetch=1,
-            grid=(steps,),
-            in_specs=[pl.BlockSpec((rows, wide), lambda g, s: (0, g))] * count
-            + [pl.BlockSpec(memory_space=pl.ANY)] * count,
-            out_specs=[spec(i) for i in range(count)],
-        ),
+        functools.partial(place_kernel, count, shards, blocks),
+        in_specs=[pl.BlockSpec(memory_space=pl.ANY)] * (2 * count),
+        out_specs=[pl.BlockSpec(memory_space=pl.ANY)] * count,
         out_shape=[jax.ShapeDtypeStruct(f.shape, f.dtype) for f in fulls],
-        input_output_aliases={1 + count + i: i for i in range(count)},
-        cost_estimate=pl.CostEstimate(flops=0, bytes_accessed=4 * count * rows * width, transcendentals=0),
+        scratch_shapes=[pltpu.SemaphoreType.DMA((count,))],
+        input_output_aliases={count + i: i for i in range(count)},
+        cost_estimate=pl.CostEstimate(flops=0, bytes_accessed=2 * count * parts[0].size, transcendentals=0),
+        compiler_params=pltpu.CompilerParams(vmem_limit_bytes=2**20),
         name="put",
-    )(blocks, *parts, *fulls)
+    )(*parts, *fulls)
 
 
 def per_device(reps, shards, weight, momentum, grad, positions):
@@ -447,57 +488,42 @@
     steps = half // WIDE
     r, s = lax.axis_index("replica"), lax.axis_index("shard")
     core = lax.rem(r, 2)
-    spread = reps % 8 == 0 and steps % 4 == 0
-    side = ((r // 2) + (r // 4)) % 2 if spread else 0 * r
-
     def ring(x, d):
         return lax.ppermute(x, "shard", [(i, (i + d) % shards) for i in range(shards)])
 
     def across(x, bit):
         return lax.ppermute(x, "replica", [(i, i ^ bit) for i in range(reps)])
 
-    others = []
-    units = np.arange(steps)
-    if spread:
-        part = half // 2
-        mine = lax.dynamic_slice(weight, (0, core * half + side * part), (rows, part))
-        for d in range(1, shards):
-            near = ring(mine, d)
-            others.append((near, across(near[:, : part // 2], 2), across(near[:, part // 2 :], 4)))
-        order = (units + side * (steps // 2)) % steps
-    else:
-        mine = lax.dynamic_slice(weight, (0, core * half), (rows, half))
-        others = [(ring(mine, d),) for d in range(1, shards)]
-        order = jnp.asarray(units)
+    mine = lax.dynamic_slice(weight, (0, core * half), (rows, half))
+    others = [ring(mine, d) for d in range(1, shards)]
 
     pos = positions[0].reshape(nx, 2 * steps, LANES)
     kept, vals, spots = own_part(momentum, grad, pos, reps, shards, topk)
 
-    def scalars(of, order):
-        base = core * steps + order
-        return jnp.concatenate([of.reshape(1), order, base, of * 2 * steps + base]).astype(jnp.int32)
+    units = np.arange(steps)
+
+    def scalars(of):
+        base = core * steps + units
+        return jnp.concatenate([of.reshape(1), jnp.asarray(units), base, of * 2 * steps + base]).astype(jnp.int32)
 
     updated, new_weight, smooth, direction, kept_full = sum_part(
-        0, scalars(s, jnp.asarray(units)), vals, spots, [(weight, True, steps)], kept, (), topk
+        0, scalars(s), vals, spots, [(weight, True, steps)], kept, (), topk
     )
-    parts = [(s, updated)]
+    parts = [updated]
     for d in range(1, shards):
         of = lax.rem(s - d + shards, shards)
-        pieces = [(w, False, w.shape[1] // WIDE) for w in others[d - 1]]
         held = (new_weight, kept_full) if d == 1 else (new_weight,)
-        out = sum_part(d, scalars(of, order), vals, spots, pieces, kept, held, topk)
+        out = sum_part(d, scalars(of), vals, spots, [(others[d - 1], False, steps)], kept, held, topk)
         updated, new_weight = out[0], out[1]
         if d == 1:
             kept_full = out[2]
-        parts.append((of, updated))
-
-    far = 1 - core
-    block = lambda *at: jnp.stack(at).astype(jnp.int32)
+        parts.append(updated)
+
     new_weight, direction = put(
-        block(s * 2 + far, far), [across(parts[0][1], 1), across(smooth, 1)], [new_weight, direction]
+        shards, [0, None], [across(parts[0], 1), across(smooth, 1)], [new_weight, direction]
     )
-    for of, piece in parts[1:]:
-        new_weight, = put(block(of * 2 + far), [across(piece, 1)], [new_weight])
+    for d in range(1, shards):
+        new_weight, = put(shards, [shards - d], [across(parts[d], 1)], [new_weight])
     return (kept_full, direction, new_weight)
 
 

time: 88.9 us -> 72.2 us (0.81)
  waiting for transfers between devices: 7.09 us -> 1.16 us
  starting transfers between devices: 9.85 us -> 5.83 us
  Pallas kernels: 63.6 us -> 60.4 us
  local copies, waits for them, and re-layouts: 5.12 us -> 2.94 us
  other arithmetic: 1.92 us -> 0.67 us
    ppermute x5 -> x3, waiting for transfers between devices: 7.09 us -> 1.16 us  [across(): return lax.ppermute(x, 'replica', [(i, i ^ bit) for i in range(reps)])]
    ppermute x5 -> x3, starting transfers between devices: 6.82 us -> 2.79 us  [across(): return lax.ppermute(x, 'replica', [(i, i ^ bit) for i in range(reps)])]
    pallas_call x2, Pallas kernels: 5.31 us -> 2.31 us  [put(): pl.pallas_call(functools.partial(place_kernel, count, shards, blocks), in...]
    unnamed x11 -> x1, local copies, waits for them, and re-layouts: 3.29 us -> 0.93 us
  transfers between devices with their start and end apart: 6 -> 4, of which waited for: 2 -> 1; matrix products, arithmetic and copies ran while one was open for 4% -> 3% of each run, Pallas kernels for 70% -> 83%
where the time goes in v4:
time: 72.2 us; the launch traced here: 71.7 us
  Pallas kernels  60.4 us (84%)
  starting transfers between devices  5.83 us (8%)
  local copies, waits for them, and re-layouts  2.94 us (4%)
  waiting for transfers between devices  1.16 us (2%)
    pallas_call x1, Pallas kernels, own_part(): pl.pallas_call(functools.partial(own_kernel, nx, topk, reps, shards), gri...  32.7 us
    pallas_call x2, Pallas kernels, sum_part(): pl.pallas_call(functools.partial(sum_kernel, nx, topk, reps, first, carri...  25.4 us
    ppermute x1, starting transfers between devices, ring(): lax.ppermute(x, 'shard', [(i, (i + d) % shards) for i in range(shards)])  3.03 us
    ppermute x3, starting transfers between devices, across(): return lax.ppermute(x, 'replica', [(i, i ^ bit) for i in range(reps)])  2.79 us
    pallas_call x2, Pallas kernels, put(): pl.pallas_call(functools.partial(place_kernel, count, shards, blocks), in...  2.31 us
  transfers between devices with their start and end apart: 4, of which 1 were waited for; matrix products, arithmetic and copies ran while one was open for 3% of the time, Pallas kernels for 83%

profile of v4, /device:TPU:0, one launch (start us, length us, event | category | flops | bytes accessed | tf_op | source)
XLA Modules:
  0.0 71.7 jit_solution(11447591413230907755)
XLA Ops:
  0.6 1.3 %constant_dynamic-slice_fusion = bf16[256,2048]{1,0:T(8,128)(2,1)S(1)} fusion(bf16[256,4096]{1,0:T(8,128)(2,1)} %refs_0_.1, s32[]{:T(128)S(6)} %select_n.3), kind=kLoop, calls=%fused_computation.5 | loop fusion | bytes 2097156 | tf_op jit(solution)/shard_map/dynamic_slice | solution.py:497
  1.9 3.0 %collective-permute-start = (bf16[256,2048]{1,0:T(8,128)(2,1)S(1)}, bf16[256,2048]{1,0:T(8,128)(2,1)}, u32[]{:S(2)}, u32[]{:S(2)}) collective-permute-start(bf16[256,2048]{1,0:T(8,128)(2,1)S(1)} %constant_dynamic-slice_fusion), channel_id=1, source_target_pairs={{0,1},{1,0},{2,3},{3,2},{4,5},{5,4},{6,7},{7,6},{8,9},{9,8},{10,11... | collective-permute-start | bytes 3145736 | tf_op jit(solution)/shard_map/ppermute | solution.py:492
  5.0 0.9 %copy.22 = s32[1,4,64,32]{3,2,1,0:T(8,128)S(1)} copy(s32[1,4,64,32]{2,3,1,0:T(8,128)} %param.16) | data formatting | bytes 65536 | tf_op args[3]
  5.9 0.7 reshape_squeeze.3.pos
  6.6 0.7 pad_add_fusion.1
  7.3 32.7 %own_part.1 = (f32[1,256,4096]{2,1,0:T(8,128)}, f32[2,16,4,8,128]{4,3,2,1,0:T(8,128)}, s16[2,16,32,128]{3,2,1,0:T(8,128)(2,1)}) custom-call(f32[1,256,4096]{2,1,0:T(8,128)} %mom.1, bf16[1,256,4096]{2,1,0:T(8,128)(2,1)} %grad.1, s32[4,16,128]{2,1,0:T(8,128)} %reshape_squeeze.3.pos, bf16[256,256]{1,0:T(8,128)(2,1)} %constant.38.clone.lf, ...), custom_call_target="tpu_custom_call" | custom-call | tf_op jit(solution)/shard_map/own_part/pallas_call | solution.py:233
  40.0 12.8 %sum_part.2 = (bf16[256,2048]{1,0:T(8,128)(2,1)}, bf16[256,8192]{1,0:T(8,128)(2,1)}, bf16[256,2048]{1,0:T(8,128)(2,1)}, bf16[256,4096]{1,0:T(8,128)(2,1)}, f32[1,256,4096]{2,1,0:T(8,128)}) custom-call(s32[25]{0:T(128)} %get-tuple-element.29.s, f32[2,16,4,8,128]{4,3,2,1,0:T(8,128)} %get-tuple-element.16.vals, ...), custom_call_target="tpu_custom_call" | custom-call | flops 16000000000 | bytes 8388608 | tf_op jit(solution)/shard_map/sum_part/pallas_call | solution.py:430
  52.8 2.2 %collective-permute-start.1 = (bf16[256,2048]{1,0:T(8,128)(2,1)}, bf16[256,2048]{1,0:T(8,128)(2,1)S(1)}, u32[]{:S(2)}, u32[]{:S(2)}) collective-permute-start(bf16[256,2048]{1,0:T(8,128)(2,1)} %get-tuple-element.22), channel_id=1, source_target_pairs={{0,2},{2,0},{4,6},{6,4},{8,10},{10,8},{12,14},{14,12},{16,18},{18,... | collective-permute-start | bytes 3145736 | tf_op jit(solution)/shard_map/ppermute | solution.py:495
  55.1 0.1 collective-permute-start.2
  55.1 0.0 collective-permute-done.refs_0_
  55.1 12.5 %sum_part.3 = (bf16[256,2048]{1,0:T(8,128)(2,1)}, bf16[256,8192]{1,0:T(8,128)(2,1)}, f32[1,256,4096]{2,1,0:T(8,128)}) custom-call(s32[25]{0:T(128)} %get-tuple-element.30.s, f32[2,16,4,8,128]{4,3,2,1,0:T(8,128)} %get-tuple-element.16.vals, s16[2,16,32,128]{3,2,1,0:T(8,128)(2,1)} %get-tuple-element.17.spots, ...), custom_call_target="tpu_custom_call", output_to_operand_aliasing={{1}: (7, {}), {2}: (8, {})} | custom-call | flops 16000000000 | bytes 8388608 | tf_op jit(solution)/shard_map/sum_part/pallas_call | solution.py:430
  67.7 0.5 collective-permute-start.3
  68.2 0.0 collective-permute-done.1.refs_0_
  68.2 0.0 collective-permute-done.2.refs_1_
  68.2 1.3 %put.2 = (bf16[256,8192]{1,0:T(8,128)(2,1)}, bf16[256,4096]{1,0:T(8,128)(2,1)}) custom-call(bf16[256,2048]{1,0:T(8,128)(2,1)S(1)} %collective-permute-done.1.refs_0_, bf16[256,2048]{1,0:T(8,128)(2,1)S(1)} %collective-permute-done.2.refs_1_, bf16[256,8192]{1,0:T(8,128)(2,1)} %get-tuple-element.24.refs_2_, ...), custom_call_target="tpu_custom_call", output_to_operand_aliasing={{0}: (2, {}), {1}: (3, {})} | custom-call | bytes 2097152 | tf_op jit(solution)/shard_map/put/pallas_call | solution.py:471
  69.5 1.2 %collective-permute-done.3.refs_0_ = bf16[256,2048]{1,0:T(8,128)(2,1)S(1)} collective-permute-done((bf16[256,2048]{1,0:T(8,128)(2,1)}, bf16[256,2048]{1,0:T(8,128)(2,1)S(1)}, u32[]{:S(2)}, u32[]{:S(2)}) %collective-permute-start.3) | collective-permute-done | bytes 1048608 | tf_op jit(solution)/shard_map/ppermute | solution.py:495
  70.7 1.0 %put.3 = bf16[256,8192]{1,0:T(8,128)(2,1)} custom-call(bf16[256,2048]{1,0:T(8,128)(2,1)S(1)} %collective-permute-done.3.refs_0_, bf16[256,8192]{1,0:T(8,128)(2,1)} %get-tuple-element.28.refs_1_), custom_call_target="tpu_custom_call", output_to_operand_aliasing={{}: (1, {})} | custom-call | bytes 1048576 | tf_op jit(solution)/shard_map/put/pallas_call | solution.py:471
  (3 shorter events, 0.0 us)
Async XLA Ops:
  1.9 53.2 %collective-permute-start = (bf16[256,2048]{1,0:T(8,128)(2,1)S(1)}, bf16[256,2048]{1,0:T(8,128)(2,1)}, u32[]{:S(2)}, u32[]{:S(2)}) collective-permute-start(bf16[256,2048]{1,0:T(8,128)(2,1)S(1)} %constant_dynamic-slice_fusion), channel_id=1, source_target_pairs={{0,1},{1,0},{2,3},{3,2},{4,5},{5,4},{6,7},{7,6},{8,9},{9,8},{10,11... | collective-permute-start | bytes 3145736 | tf_op jit(solution)/shard_map/ppermute | solution.py:492
  52.8 15.3 %collective-permute-start.1 = (bf16[256,2048]{1,0:T(8,128)(2,1)}, bf16[256,2048]{1,0:T(8,128)(2,1)S(1)}, u32[]{:S(2)}, u32[]{:S(2)}) collective-permute-start(bf16[256,2048]{1,0:T(8,128)(2,1)} %get-tuple-element.22), channel_id=1, source_target_pairs={{0,2},{2,0},{4,6},{6,4},{8,10},{10,8},{12,14},{14,12},{16,18},{18,... | collective-permute-start | bytes 3145736 | tf_op jit(solution)/shard_map/ppermute | solution.py:495
  55.1 13.1 %collective-permute-start.2 = (bf16[256,2048]{1,0:T(8,128)(2,1)}, bf16[256,2048]{1,0:T(8,128)(2,1)S(1)}, u32[]{:S(2)}, u32[]{:S(2)}) collective-permute-start(bf16[256,2048]{1,0:T(8,128)(2,1)} %get-tuple-element.23), channel_id=1, source_target_pairs={{0,2},{2,0},{4,6},{6,4},{8,10},{10,8},{12,14},{14,12},{16,18},{18,... | collective-permute-start | bytes 3145736 | tf_op jit(solution)/shard_map/ppermute | solution.py:495
  67.7 3.0 %collective-permute-start.3 = (bf16[256,2048]{1,0:T(8,128)(2,1)}, bf16[256,2048]{1,0:T(8,128)(2,1)S(1)}, u32[]{:S(2)}, u32[]{:S(2)}) collective-permute-start(bf16[256,2048]{1,0:T(8,128)(2,1)} %get-tuple-element.27), channel_id=1, source_target_pairs={{0,2},{2,0},{4,6},{6,4},{8,10},{10,8},{12,14},{14,12},{16,18},{18,... | collective-permute-start | bytes 3145736 | tf_op jit(solution)/shard_map/ppermute | solution.py:495

commit v5 on v4

--- a/solution.py
+++ b/solution.py
@@ -92,48 +92,63 @@
     return a, pos - a * GROUP + lane_offset(topk)
 
 
-def cut_points(tiles):
-    return sorted({0, tiles // 2, tiles - 1, tiles} - {-1})
-
-
-def own_kernel(nx, topk, reps, shards, mom, grad, pos, lf, rt, li, ri, kept, vals, spots, mine, at_all, places, *sems):
-    g, steps = pl.program_id(0), pl.num_programs(0)
-    lf, rt, li, ri = lf[...], rt[...], li[...], ri[...]
+def cut_points(half, tiles):
+    return sorted({0, tiles - 1, tiles}) if half else [0, tiles]
+
+
+def own_kernel(
+    nx, topk, reps, shards, mom, grad, pos, lf, rt, li, ri, kept, vals, spots,
+    mine, at_all, places, old, turned, place_send, place_recv, send_sem, recv_sem,
+):
+    g, last = pl.program_id(0), pl.num_programs(0) - 1
     tiles = mine.shape[1]
-    cuts = cut_points(tiles)
-    chunks = len(cuts) - 1
     r, s = lax.axis_index("replica"), lax.axis_index("shard")
-    me = r * shards + s
+    me = s * reps + r
     total = reps * shards
-    place_send, place_recv, place_own, send_sem, recv_sem, own_sem = sems
 
     def peer(step):
         to = lax.rem(me + step, total)
-        return to // shards, lax.rem(to, shards)
+        return lax.rem(to, reps), to // reps
 
     def place_copy(step):
         to_r, to_s = peer(step)
         return pltpu.make_async_remote_copy(
-            src_ref=places.at[lax.rem(to_r, 2)], dst_ref=spots.at[s, r],
-            send_sem=place_send.at[step], recv_sem=place_recv.at[step],
-            device_id=(to_r, to_s), device_id_type=MESH,
+            src_ref=places.at[lax.rem(to_r, 2)], dst_ref=spots.at[me],
+            send_sem=place_send, recv_sem=place_recv, device_id=(to_r, to_s), device_id_type=MESH,
         )
 
-    def value_copy(step, half, c):
-        to_r, to_s = peer(step)
-        part = pl.ds(cuts[c], cuts[c + 1] - cuts[c])
+    def value_copy(step, half, part):
+        to = lax.rem(me // 2 + step, total // 2)
+        to_s, to_r = to // (reps // 2), 2 * lax.rem(to, reps // 2) + half
         return pltpu.make_async_remote_copy(
-            src_ref=mine.at[half, part], dst_ref=vals.at[s, r, part],
-            send_sem=send_sem.at[c, step], recv_sem=recv_sem.at[c, step],
-            device_id=(to_r, to_s), device_id_type=MESH,
+            src_ref=mine.at[half, part], dst_ref=vals.at[me, part],
+            send_sem=send_sem, recv_sem=recv_sem, device_id=(to_r, to_s), device_id_type=MESH,
         )
 
-    def place_keep():
-        return pltpu.make_async_copy(places.at[lax.rem(r, 2)], spots.at[s, r], place_own)
-
-    def value_keep(half, c):
-        part = pl.ds(cuts[c], cuts[c + 1] - cuts[c])
-        return pltpu.make_async_copy(mine.at[half, part], vals.at[s, r, part], own_sem.at[c])
+    def forward():
+        moved = beta_decay * mom[0] + grad[0].astype(f32)
+        slot = lax.rem(g, 2)
+        old[slot] = moved
+        turned[slot] = right(left(lf[...], moved), rt[...])
+
+    def backward():
+        u, slot = g - 1, lax.rem(g + 1, 2)
+        a, b = place(at_all[pl.ds(pl.multiple_of(u * nx, nx), nx)], topk)
+        rows, cols = down(GROUP), down(WIDE)
+        picked, own = [], []
+        for x in range(nx):
+            part = turned[slot, x * GROUP : (x + 1) * GROUP]
+            at_row = rows == a[x : x + 1]
+            hot_a = jnp.where(at_row, 1.0, 0.0).astype(bf16)
+            hot_b = jnp.where(cols == b[x : x + 1], 1.0, 0.0).astype(bf16)
+            own.append(part * dot_t(hot_a, hot_b))
+            high, low = split(part)
+            found = dot(jnp.concatenate([high, low], axis=0), hot_b)
+            found = found[:GROUP] + found[GROUP:]
+            picked.append(jnp.sum(jnp.where(at_row, found, 0.0), axis=0, keepdims=True))
+        rows_at = pl.ds(pl.multiple_of(lax.rem(u, 2) * nx, nx), nx)
+        mine[u // (2 * tiles), lax.rem(u // 2, tiles), rows_at] = jnp.concatenate(picked, axis=0)
+        kept[0] = old[slot] - right(left(li[...], jnp.concatenate(own, axis=0)), ri[...])
 
     @pl.when(g == 0)
     def _():
@@ -148,77 +163,47 @@
         each = places.shape[1]
         for half in range(2):
             places[half] = at_all[half * each : (half + 1) * each].astype(jnp.int32).astype(jnp.int16)
-
-    moved = beta_decay * mom[0] + grad[0].astype(f32)
-    coeff = right(left(lf, moved), rt)
-    at = at_all[pl.ds(pl.multiple_of(g * nx, nx), nx)]
-    a, b = place(at, topk)
-    rows, cols = down(GROUP), down(WIDE)
-    picked, own = [], []
-    for x in range(nx):
-        part = coeff[x * GROUP : (x + 1) * GROUP]
-        at_row = rows == a[x : x + 1]
-        hot_a = jnp.where(at_row, 1.0, 0.0).astype(bf16)
-        hot_b = jnp.where(cols == b[x : x + 1], 1.0, 0.0).astype(bf16)
-        own.append(part * dot_t(hot_a, hot_b))
-        high, low = split(part)
-        found = dot(jnp.concatenate([high, low], axis=0), hot_b)
-        found = found[:GROUP] + found[GROUP:]
-        picked.append(jnp.sum(jnp.where(at_row, found, 0.0), axis=0, keepdims=True))
-    picked = jnp.concatenate(picked, axis=0)
-    half_of, tile_of = g // (2 * tiles), lax.rem(g // 2, tiles)
-    mine[half_of, tile_of, pl.ds(pl.multiple_of(lax.rem(g, 2) * nx, nx), nx)] = picked
-
-    kept[0] = moved - right(left(li, jnp.concatenate(own, axis=0)), ri)
-
-    @pl.when(g == 0)
-    def _():
-        pl.semaphore_wait(pltpu.get_barrier_semaphore(), total - 1)
-        place_keep().start()
+        forward()
+        pl.semaphore_wait(barrier, total - 1)
+        pltpu.make_async_copy(places.at[lax.rem(r, 2)], spots.at[me], place_recv).start()
 
         @pl.loop(1, total)
         def _(step):
             place_copy(step).start()
 
+    @pl.when((g > 0) & (g < last))
+    def _():
+        backward()
+        forward()
+
+    @pl.when(g == last)
+    def _():
+        backward()
+
     for half in range(2):
-        for c in range(chunks):
-            @pl.when(g == 2 * (half * tiles + cuts[c + 1]) - 1)
-            def _(half=half, c=c):
-                @pl.loop(1, total)
-                def _(step):
-                    @pl.when(lax.rem(peer(step)[0], 2) == half)
-                    def _():
-                        value_copy(step, half, c).start()
-
+        cuts = cut_points(half, tiles)
+        for begin, end in zip(cuts[:-1], cuts[1:]):
+            @pl.when(g == 2 * (half * tiles + end))
+            def _(half=half, part=pl.ds(begin, end - begin)):
                 @pl.when(lax.rem(r, 2) == half)
                 def _():
-                    value_keep(half, c).start()
-
-    @pl.when(g == steps - 1)
-    def _():
-        place_keep().wait()
-        for c in range(chunks):
-            value_keep(0, c).wait()
-
-        @pl.loop(1, total)
-        def _(step):
-            of = lax.rem(me - step + total, total)
-            of_r, of_s = of // shards, lax.rem(of, shards)
-            copy = place_copy(step)
-            copy.wait_send()
-            pltpu.make_async_remote_copy(
-                src_ref=places.at[0], dst_ref=spots.at[of_s, of_r],
-                send_sem=place_send.at[step], recv_sem=place_recv.at[step],
-                device_id=(of_r, of_s), device_id_type=MESH,
-            ).wait_recv()
-            for c in range(chunks):
-                part = pl.ds(cuts[c], cuts[c + 1] - cuts[c])
-                value_copy(step, 0, c).wait_send()
-                pltpu.make_async_remote_copy(
-                    src_ref=mine.at[0, part], dst_ref=vals.at[of_s, of_r, part],
-                    send_sem=send_sem.at[c, step], recv_sem=recv_sem.at[c, step],
-                    device_id=(of_r, of_s), device_id_type=MESH,
-                ).wait_recv()
+                    pltpu.make_async_copy(mine.at[half, part], vals.at[me, part], recv_sem).start()
+
+                @pl.when(lax.rem(r, 2) != half)
+                def _():
+                    value_copy(0, half, part).start()
+
+                @pl.loop(1, total // 2)
+                def _(step):
+                    value_copy(step, half, part).start()
+
+    @pl.when(g == last)
+    def _():
+        most = pl.ds(0, total - 1)
+        pltpu.make_async_copy(spots.at[most], spots.at[most], place_send).wait()
+        pltpu.make_async_copy(spots, spots, place_recv).wait()
+        pltpu.make_async_copy(vals.at[most], vals.at[most], send_sem).wait()
+        pltpu.make_async_copy(vals, vals, recv_sem).wait()
 
 
 def own_part(mom, grad, pos, reps, shards, topk):
@@ -226,35 +211,34 @@
     nx = rows // GROUP
     steps = width // WIDE
     tiles = steps // 4
-    chunks = len(cut_points(tiles)) - 1
     total = reps * shards
     whole = pl.BlockSpec((2 * PAIR, 2 * PAIR), lambda g: (0, 0))
+    now = pl.BlockSpec((1, rows, WIDE), lambda g: (0, 0, jnp.minimum(g, steps - 1)))
     dma = pltpu.SemaphoreType.DMA
     return pl.pallas_call(
         functools.partial(own_kernel, nx, topk, reps, shards),
-        grid=(steps,),
+        grid=(steps + 1,),
         in_specs=[
-            pl.BlockSpec((1, rows, WIDE), lambda g: (0, 0, g)),
-            pl.BlockSpec((1, rows, WIDE), lambda g: (0, 0, g)),
+            now, now,
             pl.BlockSpec(pos.shape, lambda g: (0, 0, 0)),
             whole, whole, whole, whole,
         ],
         out_specs=[
-            pl.BlockSpec((1, rows, WIDE), lambda g: (0, 0, g)),
+            pl.BlockSpec((1, rows, WIDE), lambda g: (0, 0, jnp.maximum(g - 1, 0))),
             pl.BlockSpec(memory_space=pl.ANY),
             pl.BlockSpec(memory_space=pl.ANY),
         ],
         out_shape=[
             jax.ShapeDtypeStruct((1, rows, width), f32),
-            jax.ShapeDtypeStruct((shards, reps, tiles, 2 * nx, LANES), f32),
-            jax.ShapeDtypeStruct((shards, reps, steps // 2 * nx, LANES), jnp.int16),
+            jax.ShapeDtypeStruct((total, tiles, 2 * nx, LANES), f32),
+            jax.ShapeDtypeStruct((total, steps // 2 * nx, LANES), jnp.int16),
         ],
         scratch_shapes=[
             pltpu.VMEM((2, tiles, 2 * nx, LANES), f32),
             pltpu.VMEM((steps * nx, LANES), f32),
             pltpu.VMEM((2, steps // 2 * nx, LANES), jnp.int16),
-            dma((total,)), dma((total,)), dma,
-            dma((chunks, total)), dma((chunks, total)), dma((chunks,)),
+            pltpu.VMEM((2, rows, WIDE), f32), pltpu.VMEM((2, rows, WIDE), f32),
+            dma, dma, dma, dma,
         ],
         compiler_params=pltpu.CompilerParams(has_side_effects=True, collective_id=0),
         name="own_part",
@@ -328,9 +312,9 @@
 
     def gather():
         rows = pl.ds(pl.multiple_of(lax.rem(g, 2) * nx, nx), nx)
-        tile = s[1 + g] // 2
+        tile = g // 2
         sums[lax.rem(g, 2)] = scatter(
-            nx, topk, [vals[0, r, 0, rows] for r in range(reps)], [at[r, tile, rows] for r in range(reps)]
+            nx, topk, [vals[r, 0, rows] for r in range(reps)], [at[r, tile, rows] for r in range(reps)]
         )
 
     def finish():
@@ -374,7 +358,7 @@
     @pl.when(g == 0)
     def _():
         for r in range(reps):
-            at[r] = spots[0, r].astype(jnp.int32).astype(f32).reshape(at.shape[1:])
+            at[r] = spots[r].astype(jnp.int32).astype(f32).reshape(at.shape[1:])
         gather()
 
     @pl.when((g > 0) & (g < last))
@@ -390,10 +374,9 @@
             drop(g - 1).wait()
 
 
-def sum_part(d, scalars, vals, spots, pieces, kept, held, topk):
-    rows, reps, tiles = pieces[0][0].shape[0], vals.shape[1], vals.shape[2]
+def sum_part(d, shards, scalars, vals, spots, pieces, kept, held, topk):
+    rows, reps, tiles = pieces[0][0].shape[0], vals.shape[0] // shards, vals.shape[1]
     nx = rows // GROUP
-    shards = vals.shape[0]
     steps = 2 * tiles
     width = 2 * steps * WIDE
     first, carries = d == 0, d < 2
@@ -404,17 +387,17 @@
         cut = sum(n for _, _, n in pieces[: len(cuts)])
         cuts.append(cut)
         if offset:
-            specs.append(pl.BlockSpec((rows, WIDE), lambda g, s: (0, s[1 + steps + before(g)])))
+            specs.append(pl.BlockSpec((rows, WIDE), lambda g, s: (0, s[2] + before(g))))
         else:
             specs.append(pl.BlockSpec(
                 (rows, WIDE), lambda g, s, cut=cut, n=count: (0, jnp.clip(before(g) - cut, 0, n - 1))
             ))
     whole = pl.BlockSpec((2 * PAIR, 2 * PAIR), lambda g, s: (0, 0))
-    column = lambda at: pl.BlockSpec((rows, WIDE), lambda g, s: (0, s[1 + at * steps + before(g)]))
+    column = lambda at: pl.BlockSpec((rows, WIDE), lambda g, s: (0, s[1 + at] + before(g)))
     kept_spec = pl.BlockSpec(memory_space=pl.ANY)
     in_specs = [
-        pl.BlockSpec((1, reps, 1, 2 * nx, LANES), lambda g, s: (s[0], 0, s[1 + now(g)] // 2, 0, 0)),
-        pl.BlockSpec((1,) + spots.shape[1:], lambda g, s: (s[0], 0, 0, 0)),
+        pl.BlockSpec((reps, 1, 2 * nx, LANES), lambda g, s: (s[0], now(g) // 2, 0, 0)),
+        pl.BlockSpec((reps,) + spots.shape[1:], lambda g, s: (s[0], 0, 0)),
     ] + specs + ([kept_spec] if carries else []) + [whole, whole]
     in_specs += [pl.BlockSpec(memory_space=pl.ANY)] * len(held)
     half = jax.ShapeDtypeStruct((rows, width // 2), bf16)
@@ -500,20 +483,17 @@
     pos = positions[0].reshape(nx, 2 * steps, LANES)
     kept, vals, spots = own_part(momentum, grad, pos, reps, shards, topk)
 
-    units = np.arange(steps)
-
     def scalars(of):
-        base = core * steps + units
-        return jnp.concatenate([of.reshape(1), jnp.asarray(units), base, of * 2 * steps + base]).astype(jnp.int32)
+        return jnp.stack([of, 0 * of, core * steps, (of * 2 + core) * steps]).astype(jnp.int32)
 
     updated, new_weight, smooth, direction, kept_full = sum_part(
-        0, scalars(s), vals, spots, [(weight, True, steps)], kept, (), topk
+        0, shards, scalars(s), vals, spots, [(weight, True, steps)], kept, (), topk
     )
     parts = [updated]
     for d in range(1, shards):
         of = lax.rem(s - d + shards, shards)
         held = (new_weight, kept_full) if d == 1 else (new_weight,)
-        out = sum_part(d, scalars(of), vals, spots, [(others[d - 1], False, steps)], kept, held, topk)
+        out = sum_part(d, shards, scalars(of), vals, spots, [(others[d - 1], False, steps)], kept, held, topk)
         updated, new_weight = out[0], out[1]
         if d == 1:
             kept_full = out[2]

time: 72.2 us -> 69.5 us (0.963)
  Pallas kernels: 60.4 us -> 58.5 us
  starting transfers between devices: 5.83 us -> 3.98 us
    pallas_call x1, Pallas kernels: 32.7 us -> 30.8 us  [own_part(): pl.pallas_call(functools.partial(own_kernel, nx, topk, reps, shards), gri...]
    ppermute x3, starting transfers between devices: 2.79 us -> 0.95 us  [across(): return lax.ppermute(x, 'replica', [(i, i ^ bit) for i in range(reps)])]
    another operation x0 -> x2, other arithmetic: none -> 1.31 us  [scalars(): jnp.stack([of, 0 * of, core * steps, (of * 2 + core) * steps])]
  transfers between devices with their start and end apart: 4 -> 4, of which waited for: 1 -> 1; matrix products, arithmetic and copies ran while one was open for 3% -> 4% of each run, Pallas kernels for 83% -> 84%
where the time goes in v5:
time: 69.5 us; the launch traced here: 68.6 us
  Pallas kernels  58.5 us (84%)
  starting transfers between devices  3.98 us (6%)
  local copies, waits for them, and re-layouts  2.94 us (4%)
  other arithmetic  1.31 us (2%)
  waiting for transfers between devices  1.22 us (2%)
    pallas_call x1, Pallas kernels, own_part(): pl.pallas_call(functools.partial(own_kernel, nx, topk, reps, shards), gri...  30.8 us
    pallas_call x2, Pallas kernels, sum_part(): pl.pallas_call(functools.partial(sum_kernel, nx, topk, reps, first, carri...  25.3 us
    ppermute x1, starting transfers between devices, ring(): lax.ppermute(x, 'shard', [(i, (i + d) % shards) for i in range(shards)])  3.03 us
    pallas_call x2, Pallas kernels, put(): pl.pallas_call(functools.partial(place_kernel, count, shards, blocks), in...  2.31 us
  transfers between devices with their start and end apart: 4, of which 1 were waited for; matrix products, arithmetic and copies ran while one was open for 4% of the time, Pallas kernels for 84%

profile of v5, /device:TPU:0, one launch (start us, length us, event | category | flops | bytes accessed | tf_op | source)
XLA Modules:
  0.0 68.6 jit_solution(13081553505303205088)
XLA Ops:
  0.6 1.3 %constant_dynamic-slice_fusion = bf16[256,2048]{1,0:T(8,128)(2,1)S(1)} fusion(bf16[256,4096]{1,0:T(8,128)(2,1)} %refs_0_.1, s32[]{:T(128)S(6)} %select_n.3), kind=kLoop, calls=%fused_computation.6 | loop fusion | bytes 2097156 | tf_op jit(solution)/shard_map/dynamic_slice | solution.py:480
  1.9 3.0 %collective-permute-start = (bf16[256,2048]{1,0:T(8,128)(2,1)S(1)}, bf16[256,2048]{1,0:T(8,128)(2,1)}, u32[]{:S(2)}, u32[]{:S(2)}) collective-permute-start(bf16[256,2048]{1,0:T(8,128)(2,1)S(1)} %constant_dynamic-slice_fusion), channel_id=1, source_target_pairs={{0,1},{1,0},{2,3},{3,2},{4,5},{5,4},{6,7},{7,6},{8,9},{9,8},{10,11... | collective-permute-start | bytes 3145736 | tf_op jit(solution)/shard_map/ppermute | solution.py:475
  5.0 0.9 %copy.21 = s32[1,4,64,32]{3,2,1,0:T(8,128)S(1)} copy(s32[1,4,64,32]{2,3,1,0:T(8,128)} %param.15) | data formatting | bytes 65536 | tf_op args[3]
  5.9 0.7 %reshape_squeeze.3.pos = s32[4,16,128]{2,1,0:T(8,128)} reshape(s32[1,4,64,32]{3,2,1,0:T(8,128)S(1)} %copy.21) | data formatting | bytes 65536 | tf_op jit(solution)/shard_map/reshape;squeeze | solution.py:483
  6.6 0.7 fusion.3.s
  7.3 30.8 %own_part.1 = (f32[1,256,4096]{2,1,0:T(8,128)}, f32[32,4,8,128]{3,2,1,0:T(8,128)}, s16[32,32,128]{2,1,0:T(8,128)(2,1)}) custom-call(f32[1,256,4096]{2,1,0:T(8,128)} %mom.1, bf16[1,256,4096]{2,1,0:T(8,128)(2,1)} %grad.1, s32[4,16,128]{2,1,0:T(8,128)} %reshape_squeeze.3.pos, bf16[256,256]{1,0:T(8,128)(2,1)} %constant.36.clone.lf, ...), custom_call_target="tpu_custom_call" | custom-call | tf_op jit(solution)/shard_map/own_part/pallas_call | solution.py:218
  38.1 12.9 %sum_part.2 = (bf16[256,2048]{1,0:T(8,128)(2,1)}, bf16[256,8192]{1,0:T(8,128)(2,1)}, bf16[256,2048]{1,0:T(8,128)(2,1)}, bf16[256,4096]{1,0:T(8,128)(2,1)}, f32[1,256,4096]{2,1,0:T(8,128)}) custom-call(s32[4]{0:T(128)} %fusion.3.s, f32[32,4,8,128]{3,2,1,0:T(8,128)} %get-tuple-element.16.vals, s16[32,32,128]{2,1,0:T(8,128)(2,1)} %get-tuple-element.17.spots, ...), custom_call_target="tpu_custom_call" | custom-call | flops 16000000000 | bytes 8388608 | tf_op jit(solution)/shard_map/sum_part/pallas_call | solution.py:413
  51.0 0.4 collective-permute-start.1
  51.3 0.2 collective-permute-start.2
  51.5 0.7 fusion.1.s
  52.2 0.0 collective-permute-done.refs_0_
  52.2 12.5 %sum_part.3 = (bf16[256,2048]{1,0:T(8,128)(2,1)}, bf16[256,8192]{1,0:T(8,128)(2,1)}, f32[1,256,4096]{2,1,0:T(8,128)}) custom-call(s32[4]{0:T(128)} %fusion.1.s, f32[32,4,8,128]{3,2,1,0:T(8,128)} %get-tuple-element.16.vals, s16[32,32,128]{2,1,0:T(8,128)(2,1)} %get-tuple-element.17.spots, ...), custom_call_target="tpu_custom_call", output_to_operand_aliasing={{1}: (7, {}), {2}: (8, {})} | custom-call | flops 16000000000 | bytes 8388608 | tf_op jit(solution)/shard_map/sum_part/pallas_call | solution.py:413
  64.7 0.4 collective-permute-start.3
  65.1 0.0 collective-permute-done.1.refs_0_
  65.1 0.0 collective-permute-done.2.refs_1_
  65.1 1.3 %put.2 = (bf16[256,8192]{1,0:T(8,128)(2,1)}, bf16[256,4096]{1,0:T(8,128)(2,1)}) custom-call(bf16[256,2048]{1,0:T(8,128)(2,1)S(1)} %collective-permute-done.1.refs_0_, bf16[256,2048]{1,0:T(8,128)(2,1)S(1)} %collective-permute-done.2.refs_1_, bf16[256,8192]{1,0:T(8,128)(2,1)} %get-tuple-element.24.refs_2_, ...), custom_call_target="tpu_custom_call", output_to_operand_aliasing={{0}: (2, {}), {1}: (3, {})} | custom-call | bytes 2097152 | tf_op jit(solution)/shard_map/put/pallas_call | solution.py:454
  66.4 1.2 %collective-permute-done.3.refs_0_ = bf16[256,2048]{1,0:T(8,128)(2,1)S(1)} collective-permute-done((bf16[256,2048]{1,0:T(8,128)(2,1)}, bf16[256,2048]{1,0:T(8,128)(2,1)S(1)}, u32[]{:S(2)}, u32[]{:S(2)}) %collective-permute-start.3) | collective-permute-done | bytes 1048608 | tf_op jit(solution)/shard_map/ppermute | solution.py:478
  67.6 1.0 %put.3 = bf16[256,8192]{1,0:T(8,128)(2,1)} custom-call(bf16[256,2048]{1,0:T(8,128)(2,1)S(1)} %collective-permute-done.3.refs_0_, bf16[256,8192]{1,0:T(8,128)(2,1)} %get-tuple-element.28.refs_1_), custom_call_target="tpu_custom_call", output_to_operand_aliasing={{}: (1, {})} | custom-call | bytes 1048576 | tf_op jit(solution)/shard_map/put/pallas_call | solution.py:454
Async XLA Ops:
  1.9 50.3 %collective-permute-start = (bf16[256,2048]{1,0:T(8,128)(2,1)S(1)}, bf16[256,2048]{1,0:T(8,128)(2,1)}, u32[]{:S(2)}, u32[]{:S(2)}) collective-permute-start(bf16[256,2048]{1,0:T(8,128)(2,1)S(1)} %constant_dynamic-slice_fusion), channel_id=1, source_target_pairs={{0,1},{1,0},{2,3},{3,2},{4,5},{5,4},{6,7},{7,6},{8,9},{9,8},{10,11... | collective-permute-start | bytes 3145736 | tf_op jit(solution)/shard_map/ppermute | solution.py:475
  51.0 14.1 %collective-permute-start.1 = (bf16[256,2048]{1,0:T(8,128)(2,1)}, bf16[256,2048]{1,0:T(8,128)(2,1)S(1)}, u32[]{:S(2)}, u32[]{:S(2)}) collective-permute-start(bf16[256,2048]{1,0:T(8,128)(2,1)} %get-tuple-element.22), channel_id=1, source_target_pairs={{0,2},{2,0},{4,6},{6,4},{8,10},{10,8},{12,14},{14,12},{16,18},{18,... | collective-permute-start | bytes 3145736 | tf_op jit(solution)/shard_map/ppermute | solution.py:478
  51.3 13.7 %collective-permute-start.2 = (bf16[256,2048]{1,0:T(8,128)(2,1)}, bf16[256,2048]{1,0:T(8,128)(2,1)S(1)}, u32[]{:S(2)}, u32[]{:S(2)}) collective-permute-start(bf16[256,2048]{1,0:T(8,128)(2,1)} %get-tuple-element.23), channel_id=1, source_target_pairs={{0,2},{2,0},{4,6},{6,4},{8,10},{10,8},{12,14},{14,12},{16,18},{18,... | collective-permute-start | bytes 3145736 | tf_op jit(solution)/shard_map/ppermute | solution.py:478
  64.7 2.9 %collective-permute-start.3 = (bf16[256,2048]{1,0:T(8,128)(2,1)}, bf16[256,2048]{1,0:T(8,128)(2,1)S(1)}, u32[]{:S(2)}, u32[]{:S(2)}) collective-permute-start(bf16[256,2048]{1,0:T(8,128)(2,1)} %get-tuple-element.27), channel_id=1, source_target_pairs={{0,2},{2,0},{4,6},{6,4},{8,10},{10,8},{12,14},{14,12},{16,18},{18,... | collective-permute-start | bytes 3145736 | tf_op jit(solution)/shard_map/ppermute | solution.py:478

commit v6 on v5

--- a/solution.py
+++ b/solution.py
@@ -92,8 +92,12 @@
     return a, pos - a * GROUP + lane_offset(topk)
 
 
-def cut_points(half, tiles):
-    return sorted({0, tiles - 1, tiles}) if half else [0, tiles]
+def chunks_of(tiles):
+    halves = [sorted({0, tiles // 2, tiles}), sorted({0, tiles // 2, tiles - 1, tiles})]
+    pieces = [(h, a, b) for h in range(2) for a, b in zip(halves[h][:-1], halves[h][1:])]
+    ready = [2 * (h * tiles + b) for h, _, b in pieces]
+    windows = [b - a for a, b in zip(ready[:-1], ready[1:])] + [1]
+    return list(zip(pieces, ready, windows))
 
 
 def own_kernel(
@@ -167,35 +171,41 @@
         pl.semaphore_wait(barrier, total - 1)
         pltpu.make_async_copy(places.at[lax.rem(r, 2)], spots.at[me], place_recv).start()
 
-        @pl.loop(1, total)
+    @pl.when((g > 0) & (g < last))
+    def _():
+        backward()
+        forward()
+
+    @pl.when(g == last)
+    def _():
+        backward()
+
+    share = -(-(total - 1) // tiles)
+
+    @pl.when(g < last)
+    def _():
+        @pl.loop(1 + g * share, jnp.minimum(1 + (g + 1) * share, total))
         def _(step):
             place_copy(step).start()
 
-    @pl.when((g > 0) & (g < last))
-    def _():
-        backward()
-        forward()
-
-    @pl.when(g == last)
-    def _():
-        backward()
-
-    for half in range(2):
-        cuts = cut_points(half, tiles)
-        for begin, end in zip(cuts[:-1], cuts[1:]):
-            @pl.when(g == 2 * (half * tiles + end))
-            def _(half=half, part=pl.ds(begin, end - begin)):
-                @pl.when(lax.rem(r, 2) == half)
-                def _():
-                    pltpu.make_async_copy(mine.at[half, part], vals.at[me, part], recv_sem).start()
-
-                @pl.when(lax.rem(r, 2) != half)
-                def _():
-                    value_copy(0, half, part).start()
-
-                @pl.loop(1, total // 2)
-                def _(step):
-                    value_copy(step, half, part).start()
+    for (half, begin, end), ready, window in chunks_of(tiles):
+        each = -(-(total // 2) // window)
+
+        @pl.when((g >= ready) & (g < ready + window))
+        def _(half=half, part=pl.ds(begin, end - begin), ready=ready, each=each):
+            start = (g - ready) * each
+
+            @pl.when((g == ready) & (lax.rem(r, 2) == half))
+            def _():
+                pltpu.make_async_copy(mine.at[half, part], vals.at[me, part], recv_sem).start()
+
+            @pl.when((g == ready) & (lax.rem(r, 2) != half))
+            def _():
+                value_copy(0, half, part).start()
+
+            @pl.loop(jnp.maximum(start, 1), jnp.minimum(start + each, total // 2))
+            def _(step):
+                value_copy(step, half, part).start()
 
     @pl.when(g == last)
     def _():
@@ -298,7 +308,7 @@
     return jnp.concatenate(grid, axis=0)
 
 
-def sum_kernel(nx, topk, reps, first, carries, base, cuts, held, s, vals, spots, *refs):
+def sum_kernel(nx, topk, reps, first, carries, base, cuts, held, of, near, wide, vals, spots, *refs):
     refs = list(refs)
     pieces = [refs.pop(0) for _ in cuts]
     kept_in = refs.pop(0) if carries else None
@@ -387,33 +397,34 @@
         cut = sum(n for _, _, n in pieces[: len(cuts)])
         cuts.append(cut)
         if offset:
-            specs.append(pl.BlockSpec((rows, WIDE), lambda g, s: (0, s[2] + before(g))))
+            specs.append(pl.BlockSpec((rows, WIDE), lambda g, *s: (0, s[1][0] + before(g))))
         else:
             specs.append(pl.BlockSpec(
-                (rows, WIDE), lambda g, s, cut=cut, n=count: (0, jnp.clip(before(g) - cut, 0, n - 1))
+                (rows, WIDE), lambda g, *s, cut=cut, n=count: (0, jnp.clip(before(g) - cut, 0, n - 1))
             ))
-    whole = pl.BlockSpec((2 * PAIR, 2 * PAIR), lambda g, s: (0, 0))
-    column = lambda at: pl.BlockSpec((rows, WIDE), lambda g, s: (0, s[1 + at] + before(g)))
+    whole = pl.BlockSpec((2 * PAIR, 2 * PAIR), lambda g, *s: (0, 0))
+    flat = pl.BlockSpec((rows, WIDE), lambda g, *s: (0, before(g)))
+    column = lambda at: pl.BlockSpec((rows, WIDE), lambda g, *s: (0, s[at][0] + before(g)))
     kept_spec = pl.BlockSpec(memory_space=pl.ANY)
     in_specs = [
-        pl.BlockSpec((reps, 1, 2 * nx, LANES), lambda g, s: (s[0], now(g) // 2, 0, 0)),
-        pl.BlockSpec((reps,) + spots.shape[1:], lambda g, s: (s[0], 0, 0)),
+        pl.BlockSpec((reps, 1, 2 * nx, LANES), lambda g, *s: (s[0][0], now(g) // 2, 0, 0)),
+        pl.BlockSpec((reps,) + spots.shape[1:], lambda g, *s: (s[0][0], 0, 0)),
     ] + specs + ([kept_spec] if carries else []) + [whole, whole]
     in_specs += [pl.BlockSpec(memory_space=pl.ANY)] * len(held)
     half = jax.ShapeDtypeStruct((rows, width // 2), bf16)
-    out_specs, out_shape = [column(0), column(2)], [half, jax.ShapeDtypeStruct((rows, shards * width), bf16)]
+    out_specs, out_shape = [flat, column(2)], [half, jax.ShapeDtypeStruct((rows, shards * width), bf16)]
     if first:
-        out_specs += [column(0), column(1)]
+        out_specs += [flat, column(1)]
         out_shape += [half, jax.ShapeDtypeStruct((rows, width), bf16)]
     if carries:
         out_specs.append(kept_spec)
         out_shape.append(jax.ShapeDtypeStruct((1, rows, width), f32))
-    at = 1 + len(in_specs) - len(held)
+    at = len(scalars) + len(in_specs) - len(held)
     targets = [1, 2][: len(held)]
     return pl.pallas_call(
         functools.partial(sum_kernel, nx, topk, reps, first, carries, d * steps, cuts, len(held)),
         grid_spec=pltpu.PrefetchScalarGridSpec(
-            num_scalar_prefetch=1,
+            num_scalar_prefetch=len(scalars),
             grid=(steps + 1,),
             in_specs=in_specs,
             out_specs=out_specs,
@@ -427,7 +438,7 @@
         cost_estimate=pl.CostEstimate(flops=steps * 2 * 10**9, bytes_accessed=8 * 2**20, transcendentals=0),
         name="sum_part",
     )(
-        scalars, vals, spots, *[array for array, _, _ in pieces], *([kept] if carries else []),
+        *scalars, vals, spots, *[array for array, _, _ in pieces], *([kept] if carries else []),
         left_basis(basis().T), right_basis(basis()), *held,
     )
 
@@ -477,14 +488,22 @@
     def across(x, bit):
         return lax.ppermute(x, "replica", [(i, i ^ bit) for i in range(reps)])
 
-    mine = lax.dynamic_slice(weight, (0, core * half), (rows, half))
-    others = [ring(mine, d) for d in range(1, shards)]
+    late = 3 * steps // 8 * WIDE
+    early = half - late
+    mine = lax.dynamic_slice(weight, (0, core * half), (rows, early))
+    others = [[ring(mine, d)] for d in range(1, shards)]
 
     pos = positions[0].reshape(nx, 2 * steps, LANES)
     kept, vals, spots = own_part(momentum, grad, pos, reps, shards, topk)
 
+    if late:
+        rest = lax.dynamic_slice(weight, (0, core * half + early), (rows, late))
+        rest, vals = lax.optimization_barrier((rest, vals))
+        for d in range(1, shards):
+            others[d - 1].append(ring(rest, d))
+
     def scalars(of):
-        return jnp.stack([of, 0 * of, core * steps, (of * 2 + core) * steps]).astype(jnp.int32)
+        return [v.reshape(1).astype(jnp.int32) for v in (of, core * steps, (of * 2 + core) * steps)]
 
     updated, new_weight, smooth, direction, kept_full = sum_part(
         0, shards, scalars(s), vals, spots, [(weight, True, steps)], kept, (), topk
@@ -493,7 +512,7 @@
     for d in range(1, shards):
         of = lax.rem(s - d + shards, shards)
         held = (new_weight, kept_full) if d == 1 else (new_weight,)
-        out = sum_part(d, shards, scalars(of), vals, spots, [(others[d - 1], False, steps)], kept, held, topk)
+        out = sum_part(d, shards, scalars(of), vals, spots, [(w, False, w.shape[1] // WIDE) for w in others[d - 1]], kept, held, topk)
         updated, new_weight = out[0], out[1]
         if d == 1:
             kept_full = out[2]

time: 69.5 us -> 65.5 us (0.942)
  Pallas kernels: 58.5 us -> 52.5 us
  starting transfers between devices: 3.98 us -> 5.84 us
  local copies, waits for them, and re-layouts: 2.94 us -> 4.56 us
  other arithmetic: 1.31 us -> 0 us
    pallas_call x1, Pallas kernels: 30.8 us -> 26.1 us  [own_part(): pl.pallas_call(functools.partial(own_kernel, nx, topk, reps, shards), gri...]
    ppermute x1 -> x2, starting transfers between devices: 3.03 us -> 4.49 us  [ring(): lax.ppermute(x, 'shard', [(i, (i + d) % shards) for i in range(shards)])]
    another operation x2 -> x0, other arithmetic: 1.31 us -> none  [scalars(): jnp.stack([of, 0 * of, core * steps, (of * 2 + core) * steps])]
    pallas_call x2, Pallas kernels: 25.3 us -> 24.1 us  [sum_part(): pl.pallas_call(functools.partial(sum_kernel, nx, topk, reps, first, carri...]
    dynamic_slice x1 -> x2, local copies, waits for them, and re-layouts: 1.3 us -> 2.16 us  [the longest x1 1.14 us: per_device(): mine = lax.dynamic_slice(weight, (0, core * half), (rows, early))]
    unnamed x1 -> x3, local copies, waits for them, and re-layouts: 0.93 us -> 1.7 us
  transfers between devices with their start and end apart: 4 -> 5, of which waited for: 1 -> 1; matrix products, arithmetic and copies ran while one was open for 4% -> 4% of each run, Pallas kernels for 84% -> 80%
where the time goes in v6:
time: 65.5 us; the launch traced here: 64.8 us
  Pallas kernels  52.5 us (80%)
  starting transfers between devices  5.84 us (9%)
  local copies, waits for them, and re-layouts  4.56 us (7%)
  waiting for transfers between devices  1.16 us (2%)
  between operations  0.7 us (1%)
    pallas_call x1, Pallas kernels, own_part(): pl.pallas_call(functools.partial(own_kernel, nx, topk, reps, shards), gri...  26.1 us
    pallas_call x2, Pallas kernels, sum_part(): pl.pallas_call(functools.partial(sum_kernel, nx, topk, reps, first, carri...  24.1 us
    ppermute x2, starting transfers between devices, ring(): lax.ppermute(x, 'shard', [(i, (i + d) % shards) for i in range(shards)])  4.49 us
    pallas_call x2, Pallas kernels, put(): pl.pallas_call(functools.partial(place_kernel, count, shards, blocks), in...  2.31 us
    unnamed x3, local copies, waits for them, and re-layouts  1.7 us
    ppermute x3, starting transfers between devices, across(): return lax.ppermute(x, 'replica', [(i, i ^ bit) for i in range(reps)])  1.35 us
  transfers between devices with their start and end apart: 5, of which 1 were waited for; matrix products, arithmetic and copies ran while one was open for 4% of the time, Pallas kernels for 80%

profile of v6, /device:TPU:0, one launch (start us, length us, event | category | flops | bytes accessed | tf_op | source)
XLA Modules:
  0.0 64.8 jit_solution(7825928407490978665)
XLA Ops:
  0.6 1.1 %constant_dynamic-slice_fusion = bf16[256,1280]{1,0:T(8,128)(2,1)S(1)} fusion(bf16[256,4096]{1,0:T(8,128)(2,1)} %refs_0_.1, s32[]{:T(128)S(6)} %select_n.7), kind=kLoop, calls=%fused_computation | loop fusion | bytes 1310724 | tf_op jit(solution)/shard_map/dynamic_slice | solution.py:493
  1.8 3.0 %collective-permute-start = (bf16[256,1280]{1,0:T(8,128)(2,1)S(1)}, bf16[256,1280]{1,0:T(8,128)(2,1)}, u32[]{:S(2)}, u32[]{:S(2)}) collective-permute-start(bf16[256,1280]{1,0:T(8,128)(2,1)S(1)} %constant_dynamic-slice_fusion), channel_id=1, source_target_pairs={{0,1},{1,0},{2,3},{3,2},{4,5},{5,4},{6,7},{7,6},{8,9},{9,8},{10,11... | collective-permute-start | bytes 1966088 | tf_op jit(solution)/shard_map/ppermute | solution.py:486
  4.8 0.9 %copy.21 = s32[1,4,64,32]{3,2,1,0:T(8,128)S(1)} copy(s32[1,4,64,32]{2,3,1,0:T(8,128)} %param.15) | data formatting | bytes 65536 | tf_op args[3]
  5.8 0.7 %reshape_squeeze.3.pos = s32[4,16,128]{2,1,0:T(8,128)} reshape(s32[1,4,64,32]{3,2,1,0:T(8,128)S(1)} %copy.21) | data formatting | bytes 65536 | tf_op jit(solution)/shard_map/reshape;squeeze | solution.py:496
  6.5 1.0 %constant_dynamic-slice_fusion.1 = bf16[256,768]{1,0:T(8,128)(2,1)S(1)} fusion(bf16[256,4096]{1,0:T(8,128)(2,1)} %refs_0_.1, s32[]{:T(128)S(6)} %select_n.6), kind=kLoop, calls=%fused_computation.1 | loop fusion | bytes 786436 | tf_op jit(solution)/shard_map/dynamic_slice | solution.py:500
  7.5 26.1 %own_part.1 = (f32[1,256,4096]{2,1,0:T(8,128)}, f32[32,4,8,128]{3,2,1,0:T(8,128)}, s16[32,32,128]{2,1,0:T(8,128)(2,1)}) custom-call(f32[1,256,4096]{2,1,0:T(8,128)} %mom.1, bf16[1,256,4096]{2,1,0:T(8,128)(2,1)} %grad.1, s32[4,16,128]{2,1,0:T(8,128)} %reshape_squeeze.3.pos, bf16[256,256]{1,0:T(8,128)(2,1)} %constant.38.clone.lf, ...), custom_call_target="tpu_custom_call" | custom-call | tf_op jit(solution)/shard_map/own_part/pallas_call | solution.py:228
  33.6 1.5 %collective-permute-start.1 = (bf16[256,768]{1,0:T(8,128)(2,1)S(1)}, bf16[256,768]{1,0:T(8,128)(2,1)S(1)}, u32[]{:S(2)}, u32[]{:S(2)}) collective-permute-start(bf16[256,768]{1,0:T(8,128)(2,1)S(1)} %constant_dynamic-slice_fusion.1), channel_id=1, source_target_pairs={{0,1},{1,0},{2,3},{3,2},{4,5},{5,4},{6,7},{7,6},{8,9},{9,8},{10,11... | collective-permute-start | bytes 1179656 | tf_op jit(solution)/shard_map/ppermute | solution.py:486
  35.1 12.0 %sum_part.2 = (bf16[256,2048]{1,0:T(8,128)(2,1)}, bf16[256,8192]{1,0:T(8,128)(2,1)}, bf16[256,2048]{1,0:T(8,128)(2,1)}, bf16[256,4096]{1,0:T(8,128)(2,1)}, f32[1,256,4096]{2,1,0:T(8,128)}) custom-call(s32[1]{0:T(128)} %bitcast.3.of, s32[1]{0:T(128)} %bitcast.1.near, s32[1]{0:T(128)} %bitcast.4.wide, f32[32,4,8,128]{3,2,1,0:T(8,128)} %get-tuple-element.19.vals, ...), custom_call_target="tpu_custom_call" | custom-call | flops 16000000000 | bytes 8388608 | tf_op jit(solution)/shard_map/sum_part/pallas_call | solution.py:424
  47.1 0.8 %collective-permute-start.2 = (bf16[256,2048]{1,0:T(8,128)(2,1)}, bf16[256,2048]{1,0:T(8,128)(2,1)S(1)}, u32[]{:S(2)}, u32[]{:S(2)}) collective-permute-start(bf16[256,2048]{1,0:T(8,128)(2,1)} %get-tuple-element.26), channel_id=1, source_target_pairs={{0,2},{2,0},{4,6},{6,4},{8,10},{10,8},{12,14},{14,12},{16,18},{18,... | collective-permute-start | bytes 3145736 | tf_op jit(solution)/shard_map/ppermute | solution.py:489
  47.9 0.1 collective-permute-start.3
  48.0 0.0 collective-permute-done.1.refs_1_
  48.0 0.0 copy-start
  48.0 0.0 collective-permute-done.refs_0_
  48.0 0.8 %copy-done = bf16[256,768]{1,0:T(8,128)(2,1)} copy-done((bf16[256,768]{1,0:T(8,128)(2,1)}, bf16[256,768]{1,0:T(8,128)(2,1)S(1)}, u32[]{:S(2)}) %copy-start) | copy-done | bytes 393240
  48.8 12.0 %sum_part.3 = (bf16[256,2048]{1,0:T(8,128)(2,1)}, bf16[256,8192]{1,0:T(8,128)(2,1)}, f32[1,256,4096]{2,1,0:T(8,128)}) custom-call(s32[1]{0:T(128)} %bitcast.of, s32[1]{0:T(128)} %bitcast.1.near, s32[1]{0:T(128)} %bitcast.2.wide, f32[32,4,8,128]{3,2,1,0:T(8,128)} %get-tuple-element.19.vals, ...), custom_call_target="tpu_custom_call", output_to_operand_aliasing={{1}: (10, {}), {2}: (11, {})} | custom-call | flops 16000000000 | bytes 8388608 | tf_op jit(solution)/shard_map/sum_part/pallas_call | solution.py:424
  60.8 0.5 collective-permute-start.4
  61.3 0.0 collective-permute-done.2.refs_0_
  61.3 0.0 collective-permute-done.3.refs_1_
  61.3 1.3 %put.2 = (bf16[256,8192]{1,0:T(8,128)(2,1)}, bf16[256,4096]{1,0:T(8,128)(2,1)}) custom-call(bf16[256,2048]{1,0:T(8,128)(2,1)S(1)} %collective-permute-done.2.refs_0_, bf16[256,2048]{1,0:T(8,128)(2,1)S(1)} %collective-permute-done.3.refs_1_, bf16[256,8192]{1,0:T(8,128)(2,1)} %get-tuple-element.28.refs_2_, ...), custom_call_target="tpu_custom_call", output_to_operand_aliasing={{0}: (2, {}), {1}: (3, {})} | custom-call | bytes 2097152 | tf_op jit(solution)/shard_map/put/pallas_call | solution.py:465
  62.6 1.2 %collective-permute-done.4.refs_0_ = bf16[256,2048]{1,0:T(8,128)(2,1)S(1)} collective-permute-done((bf16[256,2048]{1,0:T(8,128)(2,1)}, bf16[256,2048]{1,0:T(8,128)(2,1)S(1)}, u32[]{:S(2)}, u32[]{:S(2)}) %collective-permute-start.4) | collective-permute-done | bytes 1048608 | tf_op jit(solution)/shard_map/ppermute | solution.py:489
  63.8 1.0 %put.3 = bf16[256,8192]{1,0:T(8,128)(2,1)} custom-call(bf16[256,2048]{1,0:T(8,128)(2,1)S(1)} %collective-permute-done.4.refs_0_, bf16[256,8192]{1,0:T(8,128)(2,1)} %get-tuple-element.32.refs_1_), custom_call_target="tpu_custom_call", output_to_operand_aliasing={{}: (1, {})} | custom-call | bytes 1048576 | tf_op jit(solution)/shard_map/put/pallas_call | solution.py:465
Async XLA Ops:
  1.8 46.2 %collective-permute-start = (bf16[256,1280]{1,0:T(8,128)(2,1)S(1)}, bf16[256,1280]{1,0:T(8,128)(2,1)}, u32[]{:S(2)}, u32[]{:S(2)}) collective-permute-start(bf16[256,1280]{1,0:T(8,128)(2,1)S(1)} %constant_dynamic-slice_fusion), channel_id=1, source_target_pairs={{0,1},{1,0},{2,3},{3,2},{4,5},{5,4},{6,7},{7,6},{8,9},{9,8},{10,11... | collective-permute-start | bytes 1966088 | tf_op jit(solution)/shard_map/ppermute | solution.py:486
  33.6 14.4 %collective-permute-start.1 = (bf16[256,768]{1,0:T(8,128)(2,1)S(1)}, bf16[256,768]{1,0:T(8,128)(2,1)S(1)}, u32[]{:S(2)}, u32[]{:S(2)}) collective-permute-start(bf16[256,768]{1,0:T(8,128)(2,1)S(1)} %constant_dynamic-slice_fusion.1), channel_id=1, source_target_pairs={{0,1},{1,0},{2,3},{3,2},{4,5},{5,4},{6,7},{7,6},{8,9},{9,8},{10,11... | collective-permute-start | bytes 1179656 | tf_op jit(solution)/shard_map/ppermute | solution.py:486
  47.1 14.2 %collective-permute-start.2 = (bf16[256,2048]{1,0:T(8,128)(2,1)}, bf16[256,2048]{1,0:T(8,128)(2,1)S(1)}, u32[]{:S(2)}, u32[]{:S(2)}) collective-permute-start(bf16[256,2048]{1,0:T(8,128)(2,1)} %get-tuple-element.26), channel_id=1, source_target_pairs={{0,2},{2,0},{4,6},{6,4},{8,10},{10,8},{12,14},{14,12},{16,18},{18,... | collective-permute-start | bytes 3145736 | tf_op jit(solution)/shard_map/ppermute | solution.py:489
  47.9 13.4 %collective-permute-start.3 = (bf16[256,2048]{1,0:T(8,128)(2,1)}, bf16[256,2048]{1,0:T(8,128)(2,1)S(1)}, u32[]{:S(2)}, u32[]{:S(2)}) collective-permute-start(bf16[256,2048]{1,0:T(8,128)(2,1)} %get-tuple-element.27), channel_id=1, source_target_pairs={{0,2},{2,0},{4,6},{6,4},{8,10},{10,8},{12,14},{14,12},{16,18},{18,... | collective-permute-start | bytes 3145736 | tf_op jit(solution)/shard_map/ppermute | solution.py:489
  48.0 0.8 %copy-start = (bf16[256,768]{1,0:T(8,128)(2,1)}, bf16[256,768]{1,0:T(8,128)(2,1)S(1)}, u32[]{:S(2)}) copy-start(bf16[256,768]{1,0:T(8,128)(2,1)S(1)} %collective-permute-done.1.refs_1_) | copy-start | bytes 1179652
  60.8 3.0 %collective-permute-start.4 = (bf16[256,2048]{1,0:T(8,128)(2,1)}, bf16[256,2048]{1,0:T(8,128)(2,1)S(1)}, u32[]{:S(2)}, u32[]{:S(2)}) collective-permute-start(bf16[256,2048]{1,0:T(8,128)(2,1)} %get-tuple-element.31), channel_id=1, source_target_pairs={{0,2},{2,0},{4,6},{6,4},{8,10},{10,8},{12,14},{14,12},{16,18},{18,... | collective-permute-start | bytes 3145736 | tf_op jit(solution)/shard_map/ppermute | solution.py:489

commit v7 on v6

--- a/solution.py
+++ b/solution.py
@@ -488,7 +488,7 @@
     def across(x, bit):
         return lax.ppermute(x, "replica", [(i, i ^ bit) for i in range(reps)])
 
-    late = 3 * steps // 8 * WIDE
+    late = steps // 2 * WIDE
     early = half - late
     mine = lax.dynamic_slice(weight, (0, core * half), (rows, early))
     others = [[ring(mine, d)] for d in range(1, shards)]

time: 65.5 us -> 63.9 us (0.976)
  local copies, waits for them, and re-layouts: 4.56 us -> 2.92 us
    dynamic_slice x1 -> x0, local copies, waits for them, and re-layouts: 1.02 us -> none  [per_device(): rest = lax.dynamic_slice(weight, (0, core * half + early), (rows, late))]
    unnamed x3 -> x1, local copies, waits for them, and re-layouts: 1.7 us -> 0.93 us
  transfers between devices with their start and end apart: 5 -> 5, of which waited for: 1 -> 2; matrix products, arithmetic and copies ran while one was open for 4% -> 3% of each run, Pallas kernels for 80% -> 81%
where the time goes in v7:
time: 63.9 us; the launch traced here: 63.2 us
  Pallas kernels  52.5 us (82%)
  starting transfers between devices  5.7 us (9%)
  local copies, waits for them, and re-layouts  2.92 us (5%)
  waiting for transfers between devices  1.44 us (2%)
  between operations  0.69 us (1%)
    pallas_call x1, Pallas kernels, own_part(): pl.pallas_call(functools.partial(own_kernel, nx, topk, reps, shards), gri...  26.1 us
    pallas_call x2, Pallas kernels, sum_part(): pl.pallas_call(functools.partial(sum_kernel, nx, topk, reps, first, carri...  24.1 us
    ppermute x2, starting transfers between devices, ring(): lax.ppermute(x, 'shard', [(i, (i + d) % shards) for i in range(shards)])  4.49 us
    pallas_call x2, Pallas kernels, put(): pl.pallas_call(functools.partial(place_kernel, count, shards, blocks), in...  2.31 us
  transfers between devices with their start and end apart: 5, of which 2 were waited for; matrix products, arithmetic and copies ran while one was open for 3% of the time, Pallas kernels for 81%

profile of v7, /device:TPU:0, one launch (start us, length us, event | category | flops | bytes accessed | tf_op | source)
XLA Modules:
  0.0 63.2 jit_solution(14216493085577531340)
XLA Ops:
  0.6 1.3 %constant_dynamic-slice_fusion = (bf16[256,1024]{1,0:T(8,128)(2,1)S(1)}, bf16[256,1024]{1,0:T(8,128)(2,1)S(1)}) fusion(bf16[256,4096]{1,0:T(8,128)(2,1)} %refs_0_.1, s32[]{:T(128)S(6)} %select_n.7, s32[]{:T(128)S(6)} %select_n.6), kind=kLoop, calls=%fused_computation | loop fusion | bytes 2097160 | tf_op jit(solution)/shard_map/dynamic_slice | solution.py:493
  1.9 3.0 %collective-permute-start = (bf16[256,1024]{1,0:T(8,128)(2,1)S(1)}, bf16[256,1024]{1,0:T(8,128)(2,1)}, u32[]{:S(2)}, u32[]{:S(2)}) collective-permute-start(bf16[256,1024]{1,0:T(8,128)(2,1)S(1)} %get-tuple-element.33), channel_id=1, source_target_pairs={{0,1},{1,0},{2,3},{3,2},{4,5},{5,4},{6,7},{7,6},{8,9},{9,8},{10,11... | collective-permute-start | bytes 1572872 | tf_op jit(solution)/shard_map/ppermute | solution.py:486
  5.0 0.9 %copy.21 = s32[1,4,64,32]{3,2,1,0:T(8,128)S(1)} copy(s32[1,4,64,32]{2,3,1,0:T(8,128)} %param.15) | data formatting | bytes 65536 | tf_op args[3]
  5.9 0.7 %reshape_squeeze.3.pos = s32[4,16,128]{2,1,0:T(8,128)} reshape(s32[1,4,64,32]{3,2,1,0:T(8,128)S(1)} %copy.21) | data formatting | bytes 65536 | tf_op jit(solution)/shard_map/reshape;squeeze | solution.py:496
  6.6 26.1 %own_part.1 = (f32[1,256,4096]{2,1,0:T(8,128)}, f32[32,4,8,128]{3,2,1,0:T(8,128)}, s16[32,32,128]{2,1,0:T(8,128)(2,1)}) custom-call(f32[1,256,4096]{2,1,0:T(8,128)} %mom.1, bf16[1,256,4096]{2,1,0:T(8,128)(2,1)} %grad.1, s32[4,16,128]{2,1,0:T(8,128)} %reshape_squeeze.3.pos, bf16[256,256]{1,0:T(8,128)(2,1)} %constant.38.clone.lf, ...), custom_call_target="tpu_custom_call" | custom-call | tf_op jit(solution)/shard_map/own_part/pallas_call | solution.py:228
  32.7 1.5 %collective-permute-start.1 = (bf16[256,1024]{1,0:T(8,128)(2,1)S(1)}, bf16[256,1024]{1,0:T(8,128)(2,1)}, u32[]{:S(2)}, u32[]{:S(2)}) collective-permute-start(bf16[256,1024]{1,0:T(8,128)(2,1)S(1)} %get-tuple-element.21), channel_id=1, source_target_pairs={{0,1},{1,0},{2,3},{3,2},{4,5},{5,4},{6,7},{7,6},{8,9},{9,8},{10,11... | collective-permute-start | bytes 1572872 | tf_op jit(solution)/shard_map/ppermute | solution.py:486
  34.2 12.0 %sum_part.2 = (bf16[256,2048]{1,0:T(8,128)(2,1)}, bf16[256,8192]{1,0:T(8,128)(2,1)}, bf16[256,2048]{1,0:T(8,128)(2,1)}, bf16[256,4096]{1,0:T(8,128)(2,1)}, f32[1,256,4096]{2,1,0:T(8,128)}) custom-call(s32[1]{0:T(128)} %bitcast.3.of, s32[1]{0:T(128)} %bitcast.1.near, s32[1]{0:T(128)} %bitcast.4.wide, f32[32,4,8,128]{3,2,1,0:T(8,128)} %get-tuple-element.19.vals, ...), custom_call_target="tpu_custom_call" | custom-call | flops 16000000000 | bytes 8388608 | tf_op jit(solution)/shard_map/sum_part/pallas_call | solution.py:424
  46.2 0.8 %collective-permute-start.2 = (bf16[256,2048]{1,0:T(8,128)(2,1)}, bf16[256,2048]{1,0:T(8,128)(2,1)S(1)}, u32[]{:S(2)}, u32[]{:S(2)}) collective-permute-start(bf16[256,2048]{1,0:T(8,128)(2,1)} %get-tuple-element.26), channel_id=1, source_target_pairs={{0,2},{2,0},{4,6},{6,4},{8,10},{10,8},{12,14},{14,12},{16,18},{18,... | collective-permute-start | bytes 3145736 | tf_op jit(solution)/shard_map/ppermute | solution.py:489
  47.0 0.1 collective-permute-start.3
  47.1 0.0 collective-permute-done.refs_0_
  47.1 0.2 collective-permute-done.1.refs_1_
  47.3 12.0 %sum_part.3 = (bf16[256,2048]{1,0:T(8,128)(2,1)}, bf16[256,8192]{1,0:T(8,128)(2,1)}, f32[1,256,4096]{2,1,0:T(8,128)}) custom-call(s32[1]{0:T(128)} %bitcast.of, s32[1]{0:T(128)} %bitcast.1.near, s32[1]{0:T(128)} %bitcast.2.wide, f32[32,4,8,128]{3,2,1,0:T(8,128)} %get-tuple-element.19.vals, ...), custom_call_target="tpu_custom_call", output_to_operand_aliasing={{1}: (10, {}), {2}: (11, {})} | custom-call | flops 16000000000 | bytes 8388608 | tf_op jit(solution)/shard_map/sum_part/pallas_call | solution.py:424
  59.3 0.3 collective-permute-start.4
  59.7 0.0 collective-permute-done.2.refs_0_
  59.7 0.0 collective-permute-done.3.refs_1_
  59.7 1.3 %put.2 = (bf16[256,8192]{1,0:T(8,128)(2,1)}, bf16[256,4096]{1,0:T(8,128)(2,1)}) custom-call(bf16[256,2048]{1,0:T(8,128)(2,1)S(1)} %collective-permute-done.2.refs_0_, bf16[256,2048]{1,0:T(8,128)(2,1)S(1)} %collective-permute-done.3.refs_1_, bf16[256,8192]{1,0:T(8,128)(2,1)} %get-tuple-element.28.refs_2_, ...), custom_call_target="tpu_custom_call", output_to_operand_aliasing={{0}: (2, {}), {1}: (3, {})} | custom-call | bytes 2097152 | tf_op jit(solution)/shard_map/put/pallas_call | solution.py:465
  61.0 1.2 %collective-permute-done.4.refs_0_ = bf16[256,2048]{1,0:T(8,128)(2,1)S(1)} collective-permute-done((bf16[256,2048]{1,0:T(8,128)(2,1)}, bf16[256,2048]{1,0:T(8,128)(2,1)S(1)}, u32[]{:S(2)}, u32[]{:S(2)}) %collective-permute-start.4) | collective-permute-done | bytes 1048608 | tf_op jit(solution)/shard_map/ppermute | solution.py:489
  62.2 1.0 %put.3 = bf16[256,8192]{1,0:T(8,128)(2,1)} custom-call(bf16[256,2048]{1,0:T(8,128)(2,1)S(1)} %collective-permute-done.4.refs_0_, bf16[256,8192]{1,0:T(8,128)(2,1)} %get-tuple-element.32.refs_1_), custom_call_target="tpu_custom_call", output_to_operand_aliasing={{}: (1, {})} | custom-call | bytes 1048576 | tf_op jit(solution)/shard_map/put/pallas_call | solution.py:465
Async XLA Ops:
  1.9 45.1 %collective-permute-start = (bf16[256,1024]{1,0:T(8,128)(2,1)S(1)}, bf16[256,1024]{1,0:T(8,128)(2,1)}, u32[]{:S(2)}, u32[]{:S(2)}) collective-permute-start(bf16[256,1024]{1,0:T(8,128)(2,1)S(1)} %get-tuple-element.33), channel_id=1, source_target_pairs={{0,1},{1,0},{2,3},{3,2},{4,5},{5,4},{6,7},{7,6},{8,9},{9,8},{10,11... | collective-permute-start | bytes 1572872 | tf_op jit(solution)/shard_map/ppermute | solution.py:486
  32.7 14.6 %collective-permute-start.1 = (bf16[256,1024]{1,0:T(8,128)(2,1)S(1)}, bf16[256,1024]{1,0:T(8,128)(2,1)}, u32[]{:S(2)}, u32[]{:S(2)}) collective-permute-start(bf16[256,1024]{1,0:T(8,128)(2,1)S(1)} %get-tuple-element.21), channel_id=1, source_target_pairs={{0,1},{1,0},{2,3},{3,2},{4,5},{5,4},{6,7},{7,6},{8,9},{9,8},{10,11... | collective-permute-start | bytes 1572872 | tf_op jit(solution)/shard_map/ppermute | solution.py:486
  46.2 13.4 %collective-permute-start.2 = (bf16[256,2048]{1,0:T(8,128)(2,1)}, bf16[256,2048]{1,0:T(8,128)(2,1)S(1)}, u32[]{:S(2)}, u32[]{:S(2)}) collective-permute-start(bf16[256,2048]{1,0:T(8,128)(2,1)} %get-tuple-element.26), channel_id=1, source_target_pairs={{0,2},{2,0},{4,6},{6,4},{8,10},{10,8},{12,14},{14,12},{16,18},{18,... | collective-permute-start | bytes 3145736 | tf_op jit(solution)/shard_map/ppermute | solution.py:489
  47.0 12.7 %collective-permute-start.3 = (bf16[256,2048]{1,0:T(8,128)(2,1)}, bf16[256,2048]{1,0:T(8,128)(2,1)S(1)}, u32[]{:S(2)}, u32[]{:S(2)}) collective-permute-start(bf16[256,2048]{1,0:T(8,128)(2,1)} %get-tuple-element.27), channel_id=1, source_target_pairs={{0,2},{2,0},{4,6},{6,4},{8,10},{10,8},{12,14},{14,12},{16,18},{18,... | collective-permute-start | bytes 3145736 | tf_op jit(solution)/shard_map/ppermute | solution.py:489
  59.3 2.9 %collective-permute-start.4 = (bf16[256,2048]{1,0:T(8,128)(2,1)}, bf16[256,2048]{1,0:T(8,128)(2,1)S(1)}, u32[]{:S(2)}, u32[]{:S(2)}) collective-permute-start(bf16[256,2048]{1,0:T(8,128)(2,1)} %get-tuple-element.31), channel_id=1, source_target_pairs={{0,2},{2,0},{4,6},{6,4},{8,10},{10,8},{12,14},{14,12},{16,18},{18,... | collective-permute-start | bytes 3145736 | tf_op jit(solution)/shard_map/ppermute | solution.py:489
